TPU v7x, 256 devices: a whole 4x4x8 slice. The times are simulated.
256 devices in a mesh: unit: 4 (over z_lo), lat: 4 (over y), lon: 4 (over x_lo, core), lev: 4 (over z_hi, x_hi).
Axes of the slice: x: 4 (x_hi: 2, x_lo: 2; x = x_hi * 2 + x_lo), y: 4, z: 8 (z_hi: 2, z_lo: 4; z = z_hi * 4 + z_lo), core: 2. Of those that a mesh axis runs over, the one named last changes fastest.
Arguments:
- tracer: float32 [64, 256, 128, 128], P(('unit', 'lat'), 'lon', 'lev'), parts along dimension 0, may hold values from 0.2 to 1.8
- crowding: float32 [64, 256, 128, 128], P(('unit', 'lat'), 'lon', 'lev'), parts along dimension 0, may hold values from 0.5 to 2
Outputs:
- column_sum: float32 [64, 256, 128, 128], P(('unit', 'lat'), 'lon', 'lev'), parts along dimension 0
- tracer_end: float32 [64, 256, 128, 128], P(('unit', 'lat'), 'lon', 'lev'), parts along dimension 0
There are 4 independent parts, one for each index of `unit`. A program takes and returns all parts, laid end to end along the dimension named above; each array names one. Nothing has to cross between parts.
All inputs are finite; a program needn't handle non-finite values.
Results may differ from a plain program's by a relative error of at most 0.00002.
Values sent between devices are 32-bit elements; how exact they have to be, the bound alone decides.
A program may use at most 128 MiB of HBM per device.

v0:
```python
import jax
import jax.numpy as jnp
from jax import lax
from jax.sharding import PartitionSpec as P

STEPS = 4


def extended(array, sides, width):
    edges = {}
    for axis, dim in sides:
        devices, length = (lax.axis_size(axis), array.shape[dim])
        up = [(i, (i + 1) % devices) for i in range(devices - 1)]
        last = lax.slice_in_dim(array, length - width, length, axis=dim)
        first = lax.slice_in_dim(array, 0, width, axis=dim)
        edges[dim] = (
            lax.ppermute(last, axis, up),
            lax.ppermute(first, axis, [(b, a) for a, b in up]),
        )
    done = []
    for _, dim in sides:
        low, high = edges[dim]
        around = [(width, width) if d in done else (0, 0) for d in range(array.ndim)]
        array = jnp.concatenate([jnp.pad(low, around), array, jnp.pad(high, around)], axis=dim)
        done.append(dim)
    return array


def sent_to_all(array, axis):
    devices = lax.axis_size(axis)
    return lax.all_to_all(
        jnp.broadcast_to(array[None], (devices, *array.shape)), axis, 0, 0, tiled=True
    )


def folded_in_pairs(pieces, combine):
    while len(jax.tree.leaves(pieces)[0]) > 1:
        pieces = jax.vmap(combine)(*(pieces[side::2] for side in (0, 1)))
    return pieces[0]


def carried_in(array, axis, combine, identity):
    devices, here = (lax.axis_size(axis), lax.axis_index(axis))
    passed = jnp.arange(devices) < here

    def kept(part, zero, own):
        part = jnp.where(
            passed.reshape(-1, *(1 for _ in own.shape)), part, jnp.asarray(zero, own.dtype)
        )
        return part

    pieces = sent_to_all(array, axis)
    return folded_in_pairs(kept(pieces, identity, array), combine)


def without_rim(values, dims):
    for dim in dims:
        values = lax.slice_in_dim(values, 1, values.shape[dim] - 1, axis=dim)
    return values


def shifted_cells(values, dim, start, dims):
    others = [other for other in dims if other != dim]
    values = without_rim(values, others)
    return lax.slice_in_dim(values, start, start + values.shape[dim] - 2, axis=dim)


def march_step(padded, crowding):
    middle = without_rim(padded, (0, 1, 2))
    lower = [shifted_cells(padded, dim, 0, (0, 1, 2)) for dim in (0, 1, 2)]
    upper = [shifted_cells(padded, dim, 2, (0, 1, 2)) for dim in (0, 1, 2)]
    spread = lower[0] + upper[0] + lower[1] + upper[1] + lower[2] + upper[2] - 6.0 * middle
    return middle + 0.1 * spread + 0.2 * middle * (1.0 - middle * crowding)


def on_device(tracer, crowding):
    for step in range(STEPS):
        padded = extended(tracer, (("lat", 0), ("lon", 1), ("lev", 2)), 1)
        tracer = march_step(padded, crowding)
    here = jnp.cumsum(tracer, axis=0)
    total = lax.slice_in_dim(here, here.shape[0] - 1, here.shape[0], axis=0)

    def add_pair(earlier_total, later_total):
        return earlier_total + later_total

    below = carried_in(total, "lat", add_pair, jnp.zeros_like(total))
    column_sum = (here + below) / (tracer.shape[0] * lax.axis_size("lat"))
    return (column_sum, tracer)


def solution(mesh):
    return jax.shard_map(
        on_device,
        mesh=mesh,
        in_specs=(P(("unit", "lat"), "lon", "lev", None), P(("unit", "lat"), "lon", "lev", None)),
        out_specs=(P(("unit", "lat"), "lon", "lev", None), P(("unit", "lat"), "lon", "lev", None)),
        check_vma=False,
    )
```

profile of v0, /device:TPU:36, one launch (start us, length us, event | category | flops | bytes accessed | tf_op | source)
XLA Modules:
  0.0 231.1 jit_solution(16050239949426027099)
XLA Ops:
  0.6 4.6 %copy.14 = f32[4,64,32,128]{3,1,2,0:T(8,128)S(1)} copy(f32[4,64,32,128]{3,2,1,0:T(8,128)} %param.2) | data formatting | bytes 8388608 | tf_op args[0]
  5.3 0.2 fusion.56
  5.5 3.8 %collective-permute-start = (f32[1,64,32,128]{3,1,2,0:T(8,128)S(1)}, f32[1,64,32,128]{3,1,2,0:T(8,128)S(1)}, u32[]{:S(2)}, u32[]{:S(2)}) collective-permute-start(f32[1,64,32,128]{3,1,2,0:T(8,128)S(1)} %get-tuple-element.27), channel_id=1, source_target_pairs={{0,16},{16,32},{32,48},{1,17},{17,33},{33,49},{2,18},{18,34},{34,5... | collective-permute-start | bytes 3145736 | tf_op jit(solution)/shard_map/ppermute | solution.py:17
  9.3 1.3 collective-permute-start.1
  10.7 1.5 collective-permute-start.2
  12.1 1.3 collective-permute-start.3
  13.5 8.1 %collective-permute-start.4 = (f32[4,64,1,128]{3,1,2,0:T(8,128)S(1)}, f32[4,64,1,128]{3,1,2,0:T(8,128)S(1)}, u32[]{:S(2)}, u32[]{:S(2)}) collective-permute-start(f32[4,64,1,128]{3,1,2,0:T(8,128)S(1)} %get-tuple-element.22), channel_id=1, source_target_pairs={{0,1},{1,2},{2,3},{4,5},{5,6},{6,7},{8,9},{9,10},{10,11},{12,13},{... | collective-permute-start | bytes 393224 | tf_op jit(solution)/shard_map/ppermute | solution.py:17
  21.6 1.9 collective-permute-start.5
  23.7 8.0 %collective-permute-done = f32[1,64,32,128]{3,1,2,0:T(8,128)S(1)} collective-permute-done((f32[1,64,32,128]{3,1,2,0:T(8,128)S(1)}, f32[1,64,32,128]{3,1,2,0:T(8,128)S(1)}, u32[]{:S(2)}, u32[]{:S(2)}) %collective-permute-start) | collective-permute-done | bytes 1048608 | tf_op jit(solution)/shard_map/ppermute | solution.py:17
  31.7 0.1 constant_dynamic-update-slice_fusion.2
  31.8 2.4 %constant_dynamic-update-slice_fusion.1 = f32[6,64,32,128]{3,1,2,0:T(8,128)S(1)} fusion(f32[6,64,32,128]{3,1,2,0:T(8,128)S(1)} %constant_dynamic-update-slice_fusion.2, f32[4,64,32,128]{3,2,1,0:T(8,128)S(1)} %copy-done.4), kind=kLoop, calls=%fused_computation.117 | loop fusion | bytes 8388608
  34.2 1.6 collective-permute-done.1
  35.8 0.1 constant_dynamic-update-slice_fusion
  36.0 2.0 collective-permute-done.5
  38.0 7.4 %fusion.38 = f32[4,64,32,128]{3,1,2,0:T(8,128)S(1)} fusion(f32[4,64,32,128]{3,1,2,0:T(8,128)S(1)} %copy.14, f32[4,64,1,128]{3,1,2,0:T(8,128)S(1)} %collective-permute-done.5, f32[6,1,32,128]{3,1,2,0:T(1,128)S(1)} %pad.51, f32[6,64,32,128]{3,1,2,0:T(8,128)S(1)} %constant_dynamic-update-slice_fusion, f32[6,1,32,128]{3,1,2,0:T(1,128)S(1)} %pad.50, ...), kind=kLoop, calls=%fused_computation.93 | loop fusion | flops 31457280 | bytes 21430272 | tf_op jit(solution)/shard_map/add | solution.py:73
  45.4 0.1 fusion.52
  45.5 4.4 %collective-permute-start.6 = (f32[1,64,32,128]{3,1,2,0:T(8,128)S(1)}, f32[1,64,32,128]{3,1,2,0:T(8,128)S(1)}, u32[]{:S(2)}, u32[]{:S(2)}) collective-permute-start(f32[1,64,32,128]{3,1,2,0:T(8,128)S(1)} %get-tuple-element.18), channel_id=1, source_target_pairs={{0,16},{16,32},{32,48},{1,17},{17,33},{33,49},{2,18},{18,34},{34,5... | collective-permute-start | bytes 3145736 | tf_op jit(solution)/shard_map/ppermute | solution.py:17
  50.0 1.3 collective-permute-start.7
  51.3 0.1 fusion.53
  51.4 2.5 %collective-permute-start.8 = (f32[4,1,32,128]{3,1,2,0:T(1,128)S(1)}, f32[4,1,32,128]{3,1,2,0:T(1,128)S(1)}, u32[]{:S(2)}, u32[]{:S(2)}) collective-permute-start(f32[4,1,32,128]{3,1,2,0:T(1,128)S(1)} %get-tuple-element.20), channel_id=1, source_target_pairs={{0,4},{4,8},{8,12},{1,5},{5,9},{9,13},{2,6},{6,10},{10,14},{3,7},{... | collective-permute-start | bytes 196616 | tf_op jit(solution)/shard_map/ppermute | solution.py:17
  53.9 4.0 %collective-permute-start.10 = (f32[4,64,1,128]{3,1,2,0:T(8,128)S(1)}, f32[4,64,1,128]{3,1,2,0:T(8,128)S(1)}, u32[]{:S(2)}, u32[]{:S(2)}) collective-permute-start(f32[4,64,1,128]{3,1,2,0:T(8,128)S(1)} %get-tuple-element.16), channel_id=1, source_target_pairs={{0,1},{1,2},{2,3},{4,5},{5,6},{6,7},{8,9},{9,10},{10,11},{12,13},{... | collective-permute-start | bytes 393224 | tf_op jit(solution)/shard_map/ppermute | solution.py:17
  57.9 3.3 %collective-permute-start.11 = (f32[4,64,1,128]{3,1,2,0:T(8,128)S(1)}, f32[4,64,1,128]{3,1,2,0:T(8,128)S(1)}, u32[]{:S(2)}, u32[]{:S(2)}) collective-permute-start(f32[4,64,1,128]{3,1,2,0:T(8,128)S(1)} %get-tuple-element.17), channel_id=1, source_target_pairs={{1,0},{2,1},{3,2},{5,4},{6,5},{7,6},{9,8},{10,9},{11,10},{13,12},{... | collective-permute-start | bytes 393224 | tf_op jit(solution)/shard_map/ppermute | solution.py:18
  61.3 1.3 collective-permute-start.9
  62.6 3.9 %collective-permute-done.9 = f32[4,1,32,128]{3,1,2,0:T(1,128)S(1)} collective-permute-done((f32[4,1,32,128]{3,1,2,0:T(1,128)S(1)}, f32[4,1,32,128]{3,1,2,0:T(1,128)S(1)}, u32[]{:S(2)}, u32[]{:S(2)}) %collective-permute-start.9) | collective-permute-done | bytes 65568 | tf_op jit(solution)/shard_map/ppermute | solution.py:18
  66.6 7.7 %collective-permute-done.11 = f32[4,64,1,128]{3,1,2,0:T(8,128)S(1)} collective-permute-done((f32[4,64,1,128]{3,1,2,0:T(8,128)S(1)}, f32[4,64,1,128]{3,1,2,0:T(8,128)S(1)}, u32[]{:S(2)}, u32[]{:S(2)}) %collective-permute-start.11) | collective-permute-done | bytes 131104 | tf_op jit(solution)/shard_map/ppermute | solution.py:18
  74.4 3.1 %collective-permute-done.7 = f32[1,64,32,128]{3,1,2,0:T(8,128)S(1)} collective-permute-done((f32[1,64,32,128]{3,1,2,0:T(8,128)S(1)}, f32[1,64,32,128]{3,1,2,0:T(8,128)S(1)}, u32[]{:S(2)}, u32[]{:S(2)}) %collective-permute-start.7) | collective-permute-done | bytes 1048608 | tf_op jit(solution)/shard_map/ppermute | solution.py:18
  77.5 7.4 %fusion.27 = f32[4,64,32,128]{3,1,2,0:T(8,128)S(1)} fusion(f32[4,64,32,128]{3,1,2,0:T(8,128)S(1)} %fusion.38, f32[4,64,1,128]{3,1,2,0:T(8,128)S(1)} %collective-permute-done.11, f32[6,1,32,128]{3,1,2,0:T(1,128)S(1)} %pad.55, f32[6,1,32,128]{3,1,2,0:T(1,128)S(1)} %pad.54, f32[1,64,32,128]{3,1,2,0:T(8,128)S(1)} %collective-permute-done.7, ...), kind=kLoop, calls=%fused_computation.64 | loop fusion | flops 39845888 | bytes 15138816 | tf_op jit(solution)/shard_map/add | solution.py:73
  84.9 0.2 fusion.49
  85.2 3.4 %collective-permute-start.12 = (f32[1,64,32,128]{3,1,2,0:T(8,128)S(1)}, f32[1,64,32,128]{3,1,2,0:T(8,128)S(1)}, u32[]{:S(2)}, u32[]{:S(2)}) collective-permute-start(f32[1,64,32,128]{3,1,2,0:T(8,128)S(1)} %get-tuple-element.12), channel_id=1, source_target_pairs={{0,16},{16,32},{32,48},{1,17},{17,33},{33,49},{2,18},{18,34},{34,5... | collective-permute-start | bytes 3145736 | tf_op jit(solution)/shard_map/ppermute | solution.py:17
  88.6 1.3 collective-permute-start.13
  89.9 0.1 fusion.50
  90.0 1.3 collective-permute-start.14
  91.4 2.8 %collective-permute-start.16 = (f32[4,64,1,128]{3,1,2,0:T(8,128)S(1)}, f32[4,64,1,128]{3,1,2,0:T(8,128)S(1)}, u32[]{:S(2)}, u32[]{:S(2)}) collective-permute-start(f32[4,64,1,128]{3,1,2,0:T(8,128)S(1)} %get-tuple-element.10), channel_id=1, source_target_pairs={{0,1},{1,2},{2,3},{4,5},{5,6},{6,7},{8,9},{9,10},{10,11},{12,13},{... | collective-permute-start | bytes 393224 | tf_op jit(solution)/shard_map/ppermute | solution.py:17
  94.2 4.5 %collective-permute-start.17 = (f32[4,64,1,128]{3,1,2,0:T(8,128)S(1)}, f32[4,64,1,128]{3,1,2,0:T(8,128)S(1)}, u32[]{:S(2)}, u32[]{:S(2)}) collective-permute-start(f32[4,64,1,128]{3,1,2,0:T(8,128)S(1)} %get-tuple-element.11), channel_id=1, source_target_pairs={{1,0},{2,1},{3,2},{5,4},{6,5},{7,6},{9,8},{10,9},{11,10},{13,12},{... | collective-permute-start | bytes 393224 | tf_op jit(solution)/shard_map/ppermute | solution.py:18
  98.7 1.5 collective-permute-start.15
  100.3 1.7 collective-permute-done.15
  102.0 8.6 %collective-permute-done.17 = f32[4,64,1,128]{3,1,2,0:T(8,128)S(1)} collective-permute-done((f32[4,64,1,128]{3,1,2,0:T(8,128)S(1)}, f32[4,64,1,128]{3,1,2,0:T(8,128)S(1)}, u32[]{:S(2)}, u32[]{:S(2)}) %collective-permute-start.17) | collective-permute-done | bytes 131104 | tf_op jit(solution)/shard_map/ppermute | solution.py:18
  110.6 0.2 collective-permute-done.12
  110.8 4.2 %collective-permute-done.13 = f32[1,64,32,128]{3,1,2,0:T(8,128)S(1)} collective-permute-done((f32[1,64,32,128]{3,1,2,0:T(8,128)S(1)}, f32[1,64,32,128]{3,1,2,0:T(8,128)S(1)}, u32[]{:S(2)}, u32[]{:S(2)}) %collective-permute-start.13) | collective-permute-done | bytes 1048608 | tf_op jit(solution)/shard_map/ppermute | solution.py:18
  115.0 7.4 %fusion.16 = f32[4,64,32,128]{3,1,2,0:T(8,128)S(1)} fusion(f32[4,64,32,128]{3,1,2,0:T(8,128)S(1)} %fusion.27, f32[4,64,1,128]{3,1,2,0:T(8,128)S(1)} %collective-permute-done.17, f32[6,1,32,128]{3,1,2,0:T(1,128)S(1)} %pad.59, f32[6,1,32,128]{3,1,2,0:T(1,128)S(1)} %pad.58, f32[1,64,32,128]{3,1,2,0:T(8,128)S(1)} %collective-permute-done.13, ...), kind=kLoop, calls=%fused_computation.35 | loop fusion | flops 39845888 | bytes 15138816 | tf_op jit(solution)/shard_map/add | solution.py:73
  122.4 0.2 fusion.46
  122.6 3.3 %collective-permute-start.18 = (f32[1,64,32,128]{3,1,2,0:T(8,128)S(1)}, f32[1,64,32,128]{3,1,2,0:T(8,128)S(1)}, u32[]{:S(2)}, u32[]{:S(2)}) collective-permute-start(f32[1,64,32,128]{3,1,2,0:T(8,128)S(1)} %get-tuple-element.6), channel_id=1, source_target_pairs={{0,16},{16,32},{32,48},{1,17},{17,33},{33,49},{2,18},{18,34},{34,5... | collective-permute-start | bytes 3145736 | tf_op jit(solution)/shard_map/ppermute | solution.py:17
  125.9 1.3 collective-permute-start.19
  127.3 1.3 collective-permute-start.20
  128.6 1.9 collective-permute-start.22
  130.6 5.4 %collective-permute-start.23 = (f32[4,64,1,128]{3,1,2,0:T(8,128)S(1)}, f32[4,64,1,128]{3,1,2,0:T(8,128)S(1)}, u32[]{:S(2)}, u32[]{:S(2)}) collective-permute-start(f32[4,64,1,128]{3,1,2,0:T(8,128)S(1)} %get-tuple-element.5), channel_id=1, source_target_pairs={{1,0},{2,1},{3,2},{5,4},{6,5},{7,6},{9,8},{10,9},{11,10},{13,12},{... | collective-permute-start | bytes 393224 | tf_op jit(solution)/shard_map/ppermute | solution.py:18
  136.0 1.3 collective-permute-start.21
  137.4 1.8 collective-permute-done.21
  139.2 8.6 %collective-permute-done.23 = f32[4,64,1,128]{3,1,2,0:T(8,128)S(1)} collective-permute-done((f32[4,64,1,128]{3,1,2,0:T(8,128)S(1)}, f32[4,64,1,128]{3,1,2,0:T(8,128)S(1)}, u32[]{:S(2)}, u32[]{:S(2)}) %collective-permute-start.23) | collective-permute-done | bytes 131104 | tf_op jit(solution)/shard_map/ppermute | solution.py:18
  147.9 3.3 %collective-permute-done.19 = f32[1,64,32,128]{3,1,2,0:T(8,128)S(1)} collective-permute-done((f32[1,64,32,128]{3,1,2,0:T(8,128)S(1)}, f32[1,64,32,128]{3,1,2,0:T(8,128)S(1)}, u32[]{:S(2)}, u32[]{:S(2)}) %collective-permute-start.19) | collective-permute-done | bytes 1048608 | tf_op jit(solution)/shard_map/ppermute | solution.py:18
  151.1 7.4 %fusion.5 = f32[4,64,32,128]{3,1,2,0:T(8,128)S(1)} fusion(f32[4,64,32,128]{3,1,2,0:T(8,128)S(1)} %fusion.16, f32[4,64,1,128]{3,1,2,0:T(8,128)S(1)} %collective-permute-done.23, f32[6,1,32,128]{3,1,2,0:T(1,128)S(1)} %pad.63, f32[6,1,32,128]{3,1,2,0:T(1,128)S(1)} %pad.62, f32[1,64,32,128]{3,1,2,0:T(8,128)S(1)} %collective-permute-done.19, ...), kind=kLoop, calls=%fused_computation.6 | loop fusion | flops 39845888 | bytes 15138816 | tf_op jit(solution)/shard_map/add | solution.py:73
  158.6 2.0 copy-done.1
  160.6 3.9 %fusion.57 = f32[4,64,32,128]{3,1,2,0:T(8,128)S(1)} fusion(f32[4,64,32,128]{3,1,2,0:T(8,128)S(1)} %fusion.5), kind=kOutput, calls=%fused_computation.132 | output fusion | flops 3145728 | bytes 8388608 | tf_op jit(solution)/shard_map/jit(cumsum)/reduce_window_sum | solution.py:80
  164.5 2.0 copy-done.2
  166.6 2.6 %broadcast_in_dim.23 = f32[4,1,64,32,128]{4,2,3,1,0:T(8,128)} broadcast(f32[64,32,128]{2,0,1:T(8,128)S(1)} %slice_bitcast_fusion), dimensions={2,3,4} | broadcast | bytes 5242880 | tf_op jit(solution)/shard_map/broadcast_in_dim | solution.py:32
  169.1 4.8 %all-to-all-start = ((f32[4,1,64,32,128]{4,2,3,1,0:T(8,128)}), f32[4,1,64,32,128]{4,2,3,1,0:T(8,128)}, u32[]{:S(2)}, u32[]{:S(2)}) async-start(f32[4,1,64,32,128]{4,2,3,1,0:T(8,128)} %broadcast_in_dim.23), calls=%async_computation | async-start | bytes 8388608 | tf_op jit(solution)/shard_map/all_to_all | solution.py:31
  174.0 6.6 %copy.22 = f32[4,64,32,128]{3,2,1,0:T(8,128)} copy(f32[4,64,32,128]{3,1,2,0:T(8,128)} %copy-done.1) | data formatting | bytes 8388608
  180.6 40.1 %all-to-all-done = f32[4,1,64,32,128]{4,2,3,1,0:T(8,128)} async-done(((f32[4,1,64,32,128]{4,2,3,1,0:T(8,128)}), f32[4,1,64,32,128]{4,2,3,1,0:T(8,128)}, u32[]{:S(2)}, u32[]{:S(2)}) %all-to-all-start) | async-done | bytes 4194336 | tf_op jit(solution)/shard_map/all_to_all | solution.py:31
  220.7 2.7 %broadcast_select_fusion = f32[4,1,64,32,128]{4,2,3,1,0:T(8,128)S(1)} fusion(f32[4,1,64,32,128]{4,2,3,1,0:T(8,128)} %all-to-all-done, pred[4]{0:T(512)(128)(4,1)S(1)} %iota_compare_fusion), kind=kLoop, calls=%fused_computation.112 | loop fusion | flops 1048576 | bytes 8388612 | tf_op jit(solution)/shard_map/jit(_where)/select_n | solution.py:47
  223.4 0.4 slice_add_fusion
  223.9 0.2 fusion.44
  224.1 1.6 copy-done.3
  225.6 1.0 add_multiply_fusion
  226.7 4.4 %copy.21 = f32[4,64,32,128]{3,2,1,0:T(8,128)} copy(f32[4,64,32,128]{3,1,2,0:T(8,128)S(1)} %add_multiply_fusion) | data formatting | bytes 8388608
  (34 shorter events, 0.8 us)
Async XLA Ops:
  5.2 5.4 %copy-start.4 = (f32[4,64,32,128]{3,2,1,0:T(8,128)S(1)}, f32[4,64,32,128]{3,2,1,0:T(8,128)}, u32[]{:S(2)}) copy-start(f32[4,64,32,128]{3,2,1,0:T(8,128)} %param.2) | copy-start | bytes 12582916
  5.5 26.2 %collective-permute-start = (f32[1,64,32,128]{3,1,2,0:T(8,128)S(1)}, f32[1,64,32,128]{3,1,2,0:T(8,128)S(1)}, u32[]{:S(2)}, u32[]{:S(2)}) collective-permute-start(f32[1,64,32,128]{3,1,2,0:T(8,128)S(1)} %get-tuple-element.27), channel_id=1, source_target_pairs={{0,16},{16,32},{32,48},{1,17},{17,33},{33,49},{2,18},{18,34},{34,5... | collective-permute-start | bytes 3145736 | tf_op jit(solution)/shard_map/ppermute | solution.py:17
  9.3 26.5 %collective-permute-start.1 = (f32[1,64,32,128]{3,1,2,0:T(8,128)S(1)}, f32[1,64,32,128]{3,1,2,0:T(8,128)S(1)}, u32[]{:S(2)}, u32[]{:S(2)}) collective-permute-start(f32[1,64,32,128]{3,1,2,0:T(8,128)S(1)} %get-tuple-element.26), channel_id=1, source_target_pairs={{16,0},{32,16},{48,32},{17,1},{33,17},{49,33},{18,2},{34,18},{50,3... | collective-permute-start | bytes 3145736 | tf_op jit(solution)/shard_map/ppermute | solution.py:18
  10.7 10.9 %collective-permute-start.2 = (f32[4,1,32,128]{3,1,2,0:T(1,128)S(1)}, f32[4,1,32,128]{3,1,2,0:T(1,128)S(1)}, u32[]{:S(2)}, u32[]{:S(2)}) collective-permute-start(f32[4,1,32,128]{3,1,2,0:T(1,128)S(1)} %bitcast.8), channel_id=1, source_target_pairs={{0,4},{4,8},{8,12},{1,5},{5,9},{9,13},{2,6},{6,10},{10,14},{3,7},{... | collective-permute-start | bytes 196616 | tf_op jit(solution)/shard_map/ppermute | solution.py:17
  12.1 11.5 %collective-permute-start.3 = (f32[4,1,32,128]{3,1,2,0:T(1,128)S(1)}, f32[4,1,32,128]{3,1,2,0:T(1,128)S(1)}, u32[]{:S(2)}, u32[]{:S(2)}) collective-permute-start(f32[4,1,32,128]{3,1,2,0:T(1,128)S(1)} %bitcast.7), channel_id=1, source_target_pairs={{4,0},{8,4},{12,8},{5,1},{9,5},{13,9},{6,2},{10,6},{14,10},{7,3},{... | collective-permute-start | bytes 196616 | tf_op jit(solution)/shard_map/ppermute | solution.py:18
  13.5 22.5 %collective-permute-start.4 = (f32[4,64,1,128]{3,1,2,0:T(8,128)S(1)}, f32[4,64,1,128]{3,1,2,0:T(8,128)S(1)}, u32[]{:S(2)}, u32[]{:S(2)}) collective-permute-start(f32[4,64,1,128]{3,1,2,0:T(8,128)S(1)} %get-tuple-element.22), channel_id=1, source_target_pairs={{0,1},{1,2},{2,3},{4,5},{5,6},{6,7},{8,9},{9,10},{10,11},{12,13},{... | collective-permute-start | bytes 393224 | tf_op jit(solution)/shard_map/ppermute | solution.py:17
  21.6 16.4 %collective-permute-start.5 = (f32[4,64,1,128]{3,1,2,0:T(8,128)S(1)}, f32[4,64,1,128]{3,1,2,0:T(8,128)S(1)}, u32[]{:S(2)}, u32[]{:S(2)}) collective-permute-start(f32[4,64,1,128]{3,1,2,0:T(8,128)S(1)} %get-tuple-element.23), channel_id=1, source_target_pairs={{1,0},{2,1},{3,2},{5,4},{6,5},{7,6},{9,8},{10,9},{11,10},{13,12},{... | collective-permute-start | bytes 393224 | tf_op jit(solution)/shard_map/ppermute | solution.py:18
  31.8 6.2 %copy-start = (f32[4,64,32,128]{3,2,1,0:T(8,128)S(1)}, f32[4,64,32,128]{3,2,1,0:T(8,128)}, u32[]{:S(2)}) copy-start(f32[4,64,32,128]{3,2,1,0:T(8,128)} %param.3) | copy-start | bytes 12582916
  45.5 28.8 %collective-permute-start.6 = (f32[1,64,32,128]{3,1,2,0:T(8,128)S(1)}, f32[1,64,32,128]{3,1,2,0:T(8,128)S(1)}, u32[]{:S(2)}, u32[]{:S(2)}) collective-permute-start(f32[1,64,32,128]{3,1,2,0:T(8,128)S(1)} %get-tuple-element.18), channel_id=1, source_target_pairs={{0,16},{16,32},{32,48},{1,17},{17,33},{33,49},{2,18},{18,34},{34,5... | collective-permute-start | bytes 3145736 | tf_op jit(solution)/shard_map/ppermute | solution.py:17
  50.0 27.5 %collective-permute-start.7 = (f32[1,64,32,128]{3,1,2,0:T(8,128)S(1)}, f32[1,64,32,128]{3,1,2,0:T(8,128)S(1)}, u32[]{:S(2)}, u32[]{:S(2)}) collective-permute-start(f32[1,64,32,128]{3,1,2,0:T(8,128)S(1)} %get-tuple-element.19), channel_id=1, source_target_pairs={{16,0},{32,16},{48,32},{17,1},{33,17},{49,33},{18,2},{34,18},{50,3... | collective-permute-start | bytes 3145736 | tf_op jit(solution)/shard_map/ppermute | solution.py:18
  51.4 9.9 %collective-permute-start.8 = (f32[4,1,32,128]{3,1,2,0:T(1,128)S(1)}, f32[4,1,32,128]{3,1,2,0:T(1,128)S(1)}, u32[]{:S(2)}, u32[]{:S(2)}) collective-permute-start(f32[4,1,32,128]{3,1,2,0:T(1,128)S(1)} %get-tuple-element.20), channel_id=1, source_target_pairs={{0,4},{4,8},{8,12},{1,5},{5,9},{9,13},{2,6},{6,10},{10,14},{3,7},{... | collective-permute-start | bytes 196616 | tf_op jit(solution)/shard_map/ppermute | solution.py:17
  53.9 12.7 %collective-permute-start.10 = (f32[4,64,1,128]{3,1,2,0:T(8,128)S(1)}, f32[4,64,1,128]{3,1,2,0:T(8,128)S(1)}, u32[]{:S(2)}, u32[]{:S(2)}) collective-permute-start(f32[4,64,1,128]{3,1,2,0:T(8,128)S(1)} %get-tuple-element.16), channel_id=1, source_target_pairs={{0,1},{1,2},{2,3},{4,5},{5,6},{6,7},{8,9},{9,10},{10,11},{12,13},{... | collective-permute-start | bytes 393224 | tf_op jit(solution)/shard_map/ppermute | solution.py:17
  57.9 16.4 %collective-permute-start.11 = (f32[4,64,1,128]{3,1,2,0:T(8,128)S(1)}, f32[4,64,1,128]{3,1,2,0:T(8,128)S(1)}, u32[]{:S(2)}, u32[]{:S(2)}) collective-permute-start(f32[4,64,1,128]{3,1,2,0:T(8,128)S(1)} %get-tuple-element.17), channel_id=1, source_target_pairs={{1,0},{2,1},{3,2},{5,4},{6,5},{7,6},{9,8},{10,9},{11,10},{13,12},{... | collective-permute-start | bytes 393224 | tf_op jit(solution)/shard_map/ppermute | solution.py:18
  61.3 5.3 %collective-permute-start.9 = (f32[4,1,32,128]{3,1,2,0:T(1,128)S(1)}, f32[4,1,32,128]{3,1,2,0:T(1,128)S(1)}, u32[]{:S(2)}, u32[]{:S(2)}) collective-permute-start(f32[4,1,32,128]{3,1,2,0:T(1,128)S(1)} %get-tuple-element.21), channel_id=1, source_target_pairs={{4,0},{8,4},{12,8},{5,1},{9,5},{13,9},{6,2},{10,6},{14,10},{7,3},{... | collective-permute-start | bytes 196616 | tf_op jit(solution)/shard_map/ppermute | solution.py:18
  85.2 25.6 %collective-permute-start.12 = (f32[1,64,32,128]{3,1,2,0:T(8,128)S(1)}, f32[1,64,32,128]{3,1,2,0:T(8,128)S(1)}, u32[]{:S(2)}, u32[]{:S(2)}) collective-permute-start(f32[1,64,32,128]{3,1,2,0:T(8,128)S(1)} %get-tuple-element.12), channel_id=1, source_target_pairs={{0,16},{16,32},{32,48},{1,17},{17,33},{33,49},{2,18},{18,34},{34,5... | collective-permute-start | bytes 3145736 | tf_op jit(solution)/shard_map/ppermute | solution.py:17
  88.6 26.4 %collective-permute-start.13 = (f32[1,64,32,128]{3,1,2,0:T(8,128)S(1)}, f32[1,64,32,128]{3,1,2,0:T(8,128)S(1)}, u32[]{:S(2)}, u32[]{:S(2)}) collective-permute-start(f32[1,64,32,128]{3,1,2,0:T(8,128)S(1)} %get-tuple-element.13), channel_id=1, source_target_pairs={{16,0},{32,16},{48,32},{17,1},{33,17},{49,33},{18,2},{34,18},{50,3... | collective-permute-start | bytes 3145736 | tf_op jit(solution)/shard_map/ppermute | solution.py:18
  90.0 8.7 %collective-permute-start.14 = (f32[4,1,32,128]{3,1,2,0:T(1,128)S(1)}, f32[4,1,32,128]{3,1,2,0:T(1,128)S(1)}, u32[]{:S(2)}, u32[]{:S(2)}) collective-permute-start(f32[4,1,32,128]{3,1,2,0:T(1,128)S(1)} %get-tuple-element.14), channel_id=1, source_target_pairs={{0,4},{4,8},{8,12},{1,5},{5,9},{9,13},{2,6},{6,10},{10,14},{3,7},{... | collective-permute-start | bytes 196616 | tf_op jit(solution)/shard_map/ppermute | solution.py:17
  91.4 10.7 %collective-permute-start.16 = (f32[4,64,1,128]{3,1,2,0:T(8,128)S(1)}, f32[4,64,1,128]{3,1,2,0:T(8,128)S(1)}, u32[]{:S(2)}, u32[]{:S(2)}) collective-permute-start(f32[4,64,1,128]{3,1,2,0:T(8,128)S(1)} %get-tuple-element.10), channel_id=1, source_target_pairs={{0,1},{1,2},{2,3},{4,5},{5,6},{6,7},{8,9},{9,10},{10,11},{12,13},{... | collective-permute-start | bytes 393224 | tf_op jit(solution)/shard_map/ppermute | solution.py:17
  94.2 16.4 %collective-permute-start.17 = (f32[4,64,1,128]{3,1,2,0:T(8,128)S(1)}, f32[4,64,1,128]{3,1,2,0:T(8,128)S(1)}, u32[]{:S(2)}, u32[]{:S(2)}) collective-permute-start(f32[4,64,1,128]{3,1,2,0:T(8,128)S(1)} %get-tuple-element.11), channel_id=1, source_target_pairs={{1,0},{2,1},{3,2},{5,4},{6,5},{7,6},{9,8},{10,9},{11,10},{13,12},{... | collective-permute-start | bytes 393224 | tf_op jit(solution)/shard_map/ppermute | solution.py:18
  98.7 3.2 %collective-permute-start.15 = (f32[4,1,32,128]{3,1,2,0:T(1,128)S(1)}, f32[4,1,32,128]{3,1,2,0:T(1,128)S(1)}, u32[]{:S(2)}, u32[]{:S(2)}) collective-permute-start(f32[4,1,32,128]{3,1,2,0:T(1,128)S(1)} %get-tuple-element.15), channel_id=1, source_target_pairs={{4,0},{8,4},{12,8},{5,1},{9,5},{13,9},{6,2},{10,6},{14,10},{7,3},{... | collective-permute-start | bytes 196616 | tf_op jit(solution)/shard_map/ppermute | solution.py:18
  122.6 25.2 %collective-permute-start.18 = (f32[1,64,32,128]{3,1,2,0:T(8,128)S(1)}, f32[1,64,32,128]{3,1,2,0:T(8,128)S(1)}, u32[]{:S(2)}, u32[]{:S(2)}) collective-permute-start(f32[1,64,32,128]{3,1,2,0:T(8,128)S(1)} %get-tuple-element.6), channel_id=1, source_target_pairs={{0,16},{16,32},{32,48},{1,17},{17,33},{33,49},{2,18},{18,34},{34,5... | collective-permute-start | bytes 3145736 | tf_op jit(solution)/shard_map/ppermute | solution.py:17
  125.9 25.2 %collective-permute-start.19 = (f32[1,64,32,128]{3,1,2,0:T(8,128)S(1)}, f32[1,64,32,128]{3,1,2,0:T(8,128)S(1)}, u32[]{:S(2)}, u32[]{:S(2)}) collective-permute-start(f32[1,64,32,128]{3,1,2,0:T(8,128)S(1)} %get-tuple-element.7), channel_id=1, source_target_pairs={{16,0},{32,16},{48,32},{17,1},{33,17},{49,33},{18,2},{34,18},{50,3... | collective-permute-start | bytes 3145736 | tf_op jit(solution)/shard_map/ppermute | solution.py:18
  127.3 8.7 %collective-permute-start.20 = (f32[4,1,32,128]{3,1,2,0:T(1,128)S(1)}, f32[4,1,32,128]{3,1,2,0:T(1,128)S(1)}, u32[]{:S(2)}, u32[]{:S(2)}) collective-permute-start(f32[4,1,32,128]{3,1,2,0:T(1,128)S(1)} %get-tuple-element.8), channel_id=1, source_target_pairs={{0,4},{4,8},{8,12},{1,5},{5,9},{9,13},{2,6},{6,10},{10,14},{3,7},{... | collective-permute-start | bytes 196616 | tf_op jit(solution)/shard_map/ppermute | solution.py:17
  128.6 10.6 %collective-permute-start.22 = (f32[4,64,1,128]{3,1,2,0:T(8,128)S(1)}, f32[4,64,1,128]{3,1,2,0:T(8,128)S(1)}, u32[]{:S(2)}, u32[]{:S(2)}) collective-permute-start(f32[4,64,1,128]{3,1,2,0:T(8,128)S(1)} %get-tuple-element.4), channel_id=1, source_target_pairs={{0,1},{1,2},{2,3},{4,5},{5,6},{6,7},{8,9},{9,10},{10,11},{12,13},{... | collective-permute-start | bytes 393224 | tf_op jit(solution)/shard_map/ppermute | solution.py:17
  130.6 17.3 %collective-permute-start.23 = (f32[4,64,1,128]{3,1,2,0:T(8,128)S(1)}, f32[4,64,1,128]{3,1,2,0:T(8,128)S(1)}, u32[]{:S(2)}, u32[]{:S(2)}) collective-permute-start(f32[4,64,1,128]{3,1,2,0:T(8,128)S(1)} %get-tuple-element.5), channel_id=1, source_target_pairs={{1,0},{2,1},{3,2},{5,4},{6,5},{7,6},{9,8},{10,9},{11,10},{13,12},{... | collective-permute-start | bytes 393224 | tf_op jit(solution)/shard_map/ppermute | solution.py:18
  136.0 3.1 %collective-permute-start.21 = (f32[4,1,32,128]{3,1,2,0:T(1,128)S(1)}, f32[4,1,32,128]{3,1,2,0:T(1,128)S(1)}, u32[]{:S(2)}, u32[]{:S(2)}) collective-permute-start(f32[4,1,32,128]{3,1,2,0:T(1,128)S(1)} %get-tuple-element.9), channel_id=1, source_target_pairs={{4,0},{8,4},{12,8},{5,1},{9,5},{13,9},{6,2},{10,6},{14,10},{7,3},{... | collective-permute-start | bytes 196616 | tf_op jit(solution)/shard_map/ppermute | solution.py:18
  158.5 2.0 copy-start.1
  164.5 2.0 copy-start.2
  169.1 51.6 %all-to-all-start = ((f32[4,1,64,32,128]{4,2,3,1,0:T(8,128)}), f32[4,1,64,32,128]{4,2,3,1,0:T(8,128)}, u32[]{:S(2)}, u32[]{:S(2)}) async-start(f32[4,1,64,32,128]{4,2,3,1,0:T(8,128)} %broadcast_in_dim.23), calls=%async_computation | async-start | bytes 8388608 | tf_op jit(solution)/shard_map/all_to_all | solution.py:31
  223.4 2.2 copy-start.3
where the time goes:
time: 232 us; the launch traced here: 231 us
  waiting for transfers between devices  94.8 us (41%)
  starting transfers between devices  68.9 us (30%)
  other arithmetic  37.9 us (16%)
  local copies, waits for them, and re-layouts  28.2 us (12%)
    ppermute x12, waiting for transfers between devices, extended(): lax.ppermute(first, axis, [(b, a) for a, b in up])  46.6 us
    all_to_all x1, waiting for transfers between devices, sent_to_all(): lax.all_to_all(jnp.broadcast_to(array[None], (devices, *array.shape)), ax...  40.1 us
    ppermute x12, starting transfers between devices, extended(): lax.ppermute(last, axis, up)  38.4 us
    add x4, other arithmetic, march_step(): return middle + 0.1 * spread + 0.2 * middle * (1.0 - middle * crowding)  29.6 us
    ppermute x12, starting transfers between devices, extended(): lax.ppermute(first, axis, [(b, a) for a, b in up])  25.7 us
    unnamed x15, local copies, waits for them, and re-layouts  23.8 us
    ppermute x12, waiting for transfers between devices, extended(): lax.ppermute(last, axis, up)  8.2 us
    all_to_all x1, starting transfers between devices, sent_to_all(): lax.all_to_all(jnp.broadcast_to(array[None], (devices, *array.shape)), ax...  4.84 us
  transfers between devices with their start and end apart: 25, of which 14 were waited for; matrix products, arithmetic and copies ran while one was open for 4% of the time, Pallas kernels for 0%

commit v1 on v0

v1 whole, which is shorter than its diff:
```python
import functools

import jax
import jax.numpy as jnp
from jax import lax
from jax.experimental import pallas as pl
from jax.experimental.pallas import tpu as pltpu
from jax.sharding import PartitionSpec as P

STEPS = 4
ROWS = 4
MESH = pl.DeviceIdType.MESH
AXES = ("unit", "lat", "lon", "lev")


def march_kernel(rows, tracer, crowding, end, carried, t, c, faces, edges, total, load_sem, send_sem,
                 lat_sem, lon_sem, lev_sem, carry_sem):
    nj, ni, nk, levels = tracer.shape
    chunks = ni // (2 * rows)
    at = {axis: lax.axis_index(axis) for axis in AXES}
    size = {axis: lax.axis_size(axis) for axis in AXES}

    def has(axis, side):
        return at[axis] > 0 if side == 0 else at[axis] < size[axis] - 1

    def there(axis, side):
        return {axis: at[axis] - 1 if side == 0 else at[axis] + 1}

    def starts(m):
        return (m * rows, ni - (m + 1) * rows)

    def lat_copy(s, a, length, m, side, source=None):
        row = 0 if side == 0 else nj - 1
        if source is None:
            source = t.at[s, 1 + row, pl.ds(1 + a, length)]
        return pltpu.make_async_remote_copy(
            source, t.at[s, nj + 1 if side == 0 else 0, pl.ds(1 + a, length)],
            send_sem.at[side], lat_sem.at[s, m, 1 - side], device_id=there("lat", side), device_id_type=MESH)

    def lon_copy(s, side, source=None):
        if source is None:
            source = t.at[s, pl.ds(1, nj), 1 if side == 0 else ni]
        return pltpu.make_async_remote_copy(
            source, t.at[s, pl.ds(1, nj), ni + 1 if side == 0 else 0],
            send_sem.at[2 + side], lon_sem.at[s, 1 - side], device_id=there("lon", side), device_id_type=MESH)

    def lev_copy(s, a, length, m, side):
        return pltpu.make_async_remote_copy(
            faces.at[s, side, pl.ds(a, length)], edges.at[s, 1 - side, pl.ds(a, length)],
            send_sem.at[4 + side], lev_sem.at[s, m, 1 - side], device_id=there("lev", side), device_id_type=MESH)

    def carry_copy(a, length, n):
        return pltpu.make_async_remote_copy(
            total.at[pl.ds(a, length)], carried.at[pl.ds(a, length)],
            send_sem.at[6], carry_sem.at[n], device_id=there("lat", 1), device_id_type=MESH)

    load_t = pltpu.make_async_copy(tracer, t.at[0, pl.ds(1, nj), pl.ds(1, ni)], load_sem.at[0])
    load_c = pltpu.make_async_copy(crowding, c, load_sem.at[1])

    barrier = pltpu.get_barrier_semaphore()
    for axis in AXES[1:]:
        for side in (0, 1):
            @pl.when(has(axis, side))
            def _():
                pl.semaphore_signal(barrier, inc=1, device_id=there(axis, side), device_id_type=MESH)
    load_t.start()
    load_c.start()

    zero = jnp.zeros((nk, levels), jnp.float32)
    for side in (0, 1):
        @pl.when(jnp.logical_not(has("lat", side)))
        def _():
            @pl.loop(0, ni)
            def _(i):
                for s in range(STEPS):
                    t[s, 0 if side == 0 else nj + 1, 1 + i] = zero

            if side == 0:
                @pl.loop(0, ni)
                def _(i):
                    carried[i] = zero

        @pl.when(jnp.logical_not(has("lon", side)))
        def _():
            for s in range(STEPS):
                for j in range(nj):
                    t[s, 1 + j, 0 if side == 0 else ni + 1] = zero

        @pl.when(jnp.logical_not(has("lev", side)))
        def _():
            @pl.loop(0, ni)
            def _(i):
                for s in range(STEPS):
                    for j in range(nj):
                        edges[s, side, i, j] = jnp.zeros((1, levels), jnp.float32)

    neighbours = sum(
        has(axis, side).astype(jnp.int32) for axis in AXES[1:] for side in (0, 1))
    pl.semaphore_wait(barrier, neighbours)

    for m in range(chunks):
        for side in (0, 1):
            @pl.when(has("lat", side))
            def _():
                for a in starts(m):
                    lat_copy(0, a, rows, m, side,
                             tracer.at[0 if side == 0 else nj - 1, pl.ds(a, rows)]).start()
    for side in (0, 1):
        @pl.when(has("lon", side))
        def _():
            lon_copy(0, side, tracer.at[:, 0 if side == 0 else ni - 1]).start()

    def send_lev(s, m):
        for side in (0, 1):
            @pl.when(has("lev", side))
            def _():
                for a in starts(m):
                    lev_copy(s, a, rows, m, side).start()

    load_t.wait()

    @pl.loop(0, chunks)
    def _(m):
        @pl.loop(0, rows)
        def _(r):
            for a in starts(m):
                for j in range(nj):
                    faces[0, 0, a + r, j] = t[0, 1 + j, 1 + a + r, 0:1]
                    faces[0, 1, a + r, j] = t[0, 1 + j, 1 + a + r, nk - 1:nk]
        send_lev(0, m)

    load_c.wait()

    below = lax.broadcasted_iota(jnp.int32, (nk, levels), 0) == 0
    above = lax.broadcasted_iota(jnp.int32, (nk, levels), 0) == nk - 1

    def stepped(s, i):
        for j in range(nj):
            middle = t[s, 1 + j, 1 + i]
            lower = jnp.where(below, edges[s, 0, i, j], pltpu.roll(middle, 1, 0))
            upper = jnp.where(above, edges[s, 1, i, j], pltpu.roll(middle, nk - 1, 0))
            spread = (t[s, j, 1 + i] + t[s, 2 + j, 1 + i] + t[s, 1 + j, i] + t[s, 1 + j, 2 + i]
                      + lower + upper - 6.0 * middle)
            yield j, middle + 0.1 * spread + 0.2 * middle * (1.0 - middle * c[j, i])

    def arrived(s, m):
        for side in (0, 1):
            @pl.when(has("lat", side))
            def _():
                lat_copy(s, 0, 2 * rows, m, 1 - side).wait_recv()

            @pl.when(has("lev", side))
            def _():
                lev_copy(s, 0, 2 * rows, m, 1 - side).wait_recv()

            @pl.when(jnp.logical_and(has("lon", side), m == 0))
            def _():
                lon_copy(s, 1 - side).wait_recv()

    @pl.loop(0, STEPS - 1)
    def _(s):
        @pl.loop(0, chunks)
        def _(m):
            arrived(s, m)

            @pl.loop(0, rows)
            def _(r):
                for a in starts(m):
                    for j, value in stepped(s, a + r):
                        t[s + 1, 1 + j, 1 + a + r] = value
                        faces[s + 1, 0, a + r, j] = value[0:1]
                        faces[s + 1, 1, a + r, j] = value[nk - 1:nk]

            for side in (0, 1):
                @pl.when(has("lat", side))
                def _():
                    for a in starts(m):
                        lat_copy(s + 1, a, rows, m, side).start()
            send_lev(s + 1, m)
            for side in (0, 1):
                @pl.when(jnp.logical_and(has("lon", side), m == 0))
                def _():
                    lon_copy(s + 1, side).start()

    first = at["lat"] == 0

    @pl.loop(0, chunks)
    def _(m):
        arrived(STEPS - 1, m)

        @pl.loop(0, rows)
        def _(r):
            for a in starts(m):
                summed = None
                for j, value in stepped(STEPS - 1, a + r):
                    end[j, a + r] = value
                    summed = value if j == 0 else summed + value
                total[a + r] = summed

        @pl.when(first)
        def _():
            for n, a in enumerate(starts(m)):
                carry_copy(a, rows, 2 * m + n).start()

    @pl.when(jnp.logical_not(first))
    def _():
        @pl.loop(0, chunks)
        def _(m):
            for n, a in enumerate(starts(m)):
                carry_copy(a, rows, 2 * m + n).wait_recv()

                @pl.when(has("lat", 1))
                def _():
                    @pl.loop(0, rows)
                    def _(r):
                        total[a + r] = total[a + r] + carried[a + r]
                    carry_copy(a, rows, 2 * m + n).start()

    for side in (0, 1):
        @pl.when(has("lat", side))
        def _():
            for s in range(STEPS):
                lat_copy(s, 0, ni, 0, side).wait_send()

        @pl.when(has("lon", side))
        def _():
            for s in range(STEPS):
                lon_copy(s, side).wait_send()

        @pl.when(has("lev", side))
        def _():
            for s in range(STEPS):
                lev_copy(s, 0, ni, 0, side).wait_send()

    @pl.when(has("lat", 1))
    def _():
        carry_copy(0, ni, 0).wait_send()


def march(tracer, crowding, rows):
    nj, ni, nk, levels = tracer.shape
    chunks = ni // (2 * rows)
    f32 = jnp.float32
    dma = pltpu.SemaphoreType.DMA
    return pl.pallas_call(
        functools.partial(march_kernel, rows),
        out_shape=(jax.ShapeDtypeStruct(tracer.shape, f32), jax.ShapeDtypeStruct(tracer.shape[1:], f32)),
        in_specs=[pl.BlockSpec(memory_space=pl.ANY)] * 2,
        out_specs=(pl.BlockSpec(memory_space=pltpu.VMEM),) * 2,
        scratch_shapes=[
            pltpu.VMEM((STEPS, nj + 2, ni + 2, nk, levels), f32),
            pltpu.VMEM((nj, ni, nk, levels), f32),
            pltpu.VMEM((STEPS, 2, ni, nj, 1, levels), f32),
            pltpu.VMEM((STEPS, 2, ni, nj, 1, levels), f32),
            pltpu.VMEM((ni, nk, levels), f32),
            dma((2,)),
            dma((7,)),
            dma((STEPS, chunks, 2)),
            dma((STEPS, 2)),
            dma((STEPS, chunks, 2)),
            dma((2 * chunks,)),
        ],
        compiler_params=pltpu.CompilerParams(
            collective_id=0, has_side_effects=True, vmem_limit_bytes=48 * 2**20),
        name="march",
    )(tracer, crowding)


def sums_kernel(scale, end, carried, sums, copied):
    run = carried[...]
    for j in range(end.shape[0]):
        value = end[j]
        run = run + value
        sums[j] = run * scale
        copied[j] = value


def sums_along_j(end, carried, cells):
    nj, ni, nk, levels = end.shape
    block = min(8, ni)
    whole = pl.BlockSpec((nj, block, nk, levels), lambda i: (0, i, 0, 0))
    return pl.pallas_call(
        functools.partial(sums_kernel, 1.0 / cells),
        grid=(ni // block,),
        out_shape=(jax.ShapeDtypeStruct(end.shape, end.dtype),) * 2,
        in_specs=[whole, pl.BlockSpec((block, nk, levels), lambda i: (i, 0, 0))],
        out_specs=(whole, whole),
        compiler_params=pltpu.CompilerParams(vmem_limit_bytes=12 * 2**20),
        name="sums",
    )(end, carried)


def on_device(tracer, crowding):
    end, carried = march(tracer, crowding, min(ROWS, tracer.shape[1] // 2))
    return sums_along_j(end, carried, tracer.shape[0] * lax.axis_size("lat"))


def solution(mesh):
    spec = P(("unit", "lat"), "lon", "lev", None)
    return jax.shard_map(
        on_device, mesh=mesh, in_specs=(spec, spec), out_specs=(spec, spec), check_vma=False)
```

time: 232 us -> 135 us (0.58)
  the two profiles are of different devices: /device:TPU:36 before, /device:TPU:30 now
where the time goes in v1:
time: 135 us
  Pallas kernels  134 us (99%)
    pallas_call x1, Pallas kernels, march(): pl.pallas_call(functools.partial(march_kernel, rows), out_shape=(jax.Shap...  129 us
    pallas_call x1, Pallas kernels, sums_along_j(): pl.pallas_call(functools.partial(sums_kernel, 1.0 / cells), grid=(ni // b...  4.65 us

profile of v1, /device:TPU:30, one launch (start us, length us, event | category | flops | bytes accessed | tf_op | source)
XLA Modules:
  0.0 134.6 jit_solution(11973220628278918922)
XLA Ops:
  0.6 129.3 %march.1 = (f32[4,64,32,128]{3,2,1,0:T(8,128)S(1)}, f32[64,32,128]{2,1,0:T(8,128)S(1)}) custom-call(f32[4,64,32,128]{3,2,1,0:T(8,128)} %tracer.1, f32[4,64,32,128]{3,2,1,0:T(8,128)} %crowding.1), custom_call_target="tpu_custom_call" | custom-call | tf_op jit(solution)/shard_map/march/pallas_call | solution.py:245
  129.9 4.7 %sums.1 = (f32[4,64,32,128]{3,2,1,0:T(8,128)}, f32[4,64,32,128]{3,2,1,0:T(8,128)}) custom-call(f32[4,64,32,128]{3,2,1,0:T(8,128)S(1)} %get-tuple-element.4.end, f32[64,32,128]{2,1,0:T(8,128)S(1)} %get-tuple-element.5.carried), custom_call_target="tpu_custom_call" | custom-call | tf_op jit(solution)/shard_map/sums/pallas_call | solution.py:282

commit v2 on v1

--- a/solution.py
+++ b/solution.py
@@ -9,12 +9,14 @@
 
 STEPS = 4
 ROWS = 4
+AROUND = 6
+RETURNED = 3
 MESH = pl.DeviceIdType.MESH
 AXES = ("unit", "lat", "lon", "lev")
 
 
-def march_kernel(rows, tracer, crowding, end, carried, t, c, faces, edges, total, load_sem, send_sem,
-                 lat_sem, lon_sem, lev_sem, carry_sem):
+def march_kernel(rows, tracer, crowding, end, carried, t, c, faces, edges, total, suffix, whole,
+                 load_sem, send_sem, lat_sem, lon_sem, lev_sem, carry_sem, suffix_sem, whole_sem):
     nj, ni, nk, levels = tracer.shape
     chunks = ni // (2 * rows)
     at = {axis: lax.axis_index(axis) for axis in AXES}
@@ -49,20 +51,51 @@
             faces.at[s, side, pl.ds(a, length)], edges.at[s, 1 - side, pl.ds(a, length)],
             send_sem.at[4 + side], lev_sem.at[s, m, 1 - side], device_id=there("lev", side), device_id_type=MESH)
 
-    def carry_copy(a, length, n):
-        return pltpu.make_async_remote_copy(
-            total.at[pl.ds(a, length)], carried.at[pl.ds(a, length)],
-            send_sem.at[6], carry_sem.at[n], device_id=there("lat", 1), device_id_type=MESH)
+    pieces = 2 * chunks
+    last = size["lat"] - 1
+
+    def span(p, count=1):
+        m = p // 2
+        return pl.ds(jnp.where(p % 2 == 0, m * rows, ni - (m + 1) * rows), count * rows)
+
+    def carry_copy(p, count=1):
+        at_p = span(p) if count == 1 else pl.ds(0, count * rows)
+        return pltpu.make_async_remote_copy(
+            total.at[at_p], carried.at[at_p], send_sem.at[6], carry_sem.at[p],
+            device_id=there("lat", 1), device_id_type=MESH)
+
+    def suffix_copy(p, source, count=1):
+        at_p = span(p) if count == 1 else pl.ds(0, count * rows)
+        return pltpu.make_async_remote_copy(
+            source.at[at_p], suffix.at[at_p], send_sem.at[7], suffix_sem.at[p],
+            device_id=there("lat", 0), device_id_type=MESH)
+
+    def round_copy(p, count=1):
+        at_p = span(p) if count == 1 else pl.ds(0, count * rows)
+        return pltpu.make_async_remote_copy(
+            suffix.at[at_p], carried.at[at_p], send_sem.at[8], carry_sem.at[p],
+            device_id={"lat": last}, device_id_type=MESH)
+
+    def whole_copy(p, source, count=1):
+        at_p = span(p) if count == 1 else pl.ds(0, count * rows)
+        return pltpu.make_async_remote_copy(
+            source.at[at_p], whole.at[at_p], send_sem.at[9], whole_sem.at[p],
+            device_id=there("lat", 0), device_id_type=MESH)
 
     load_t = pltpu.make_async_copy(tracer, t.at[0, pl.ds(1, nj), pl.ds(1, ni)], load_sem.at[0])
     load_c = pltpu.make_async_copy(crowding, c, load_sem.at[1])
 
     barrier = pltpu.get_barrier_semaphore()
-    for axis in AXES[1:]:
+
+    def greet(axis, side, where=None):
+        pl.semaphore_signal(
+            barrier, inc=1, device_id=there(axis, side) if where is None else where, device_id_type=MESH)
+
+    for axis in ("lat", "lon"):
         for side in (0, 1):
-            @pl.when(has(axis, side))
-            def _():
-                pl.semaphore_signal(barrier, inc=1, device_id=there(axis, side), device_id_type=MESH)
+            pl.when(has(axis, side))(functools.partial(greet, axis, side))
+    ends = jnp.logical_or(at["lat"] == 0, at["lat"] == last)
+    pl.when(ends)(functools.partial(greet, "lat", 0, {"lat": last - at["lat"]}))
     load_t.start()
     load_c.start()
 
@@ -94,9 +127,12 @@
                     for j in range(nj):
                         edges[s, side, i, j] = jnp.zeros((1, levels), jnp.float32)
 
-    neighbours = sum(
-        has(axis, side).astype(jnp.int32) for axis in AXES[1:] for side in (0, 1))
-    pl.semaphore_wait(barrier, neighbours)
+    def count(axis):
+        return has(axis, 0).astype(jnp.int32) + has(axis, 1).astype(jnp.int32)
+
+    odd = at["lev"] % 2 == 1
+    near = count("lat") + count("lon") + ends.astype(jnp.int32)
+    pl.semaphore_wait(barrier, near + jnp.where(odd, 0, count("lev")))
 
     for m in range(chunks):
         for side in (0, 1):
@@ -109,6 +145,9 @@
         @pl.when(has("lon", side))
         def _():
             lon_copy(0, side, tracer.at[:, 0 if side == 0 else ni - 1]).start()
+
+    for side in (0, 1):
+        pl.when(has("lev", side))(functools.partial(greet, "lev", side))
 
     def send_lev(s, m):
         for side in (0, 1):
@@ -127,6 +166,13 @@
                 for j in range(nj):
                     faces[0, 0, a + r, j] = t[0, 1 + j, 1 + a + r, 0:1]
                     faces[0, 1, a + r, j] = t[0, 1 + j, 1 + a + r, nk - 1:nk]
+
+    @pl.when(odd)
+    def _():
+        pl.semaphore_wait(barrier, count("lev"))
+
+    @pl.loop(0, chunks)
+    def _(m):
         send_lev(0, m)
 
     load_c.wait()
@@ -182,7 +228,8 @@
                 def _():
                     lon_copy(s + 1, side).start()
 
-    first = at["lat"] == 0
+    def block(n):
+        return pl.when(at["lat"] == n)
 
     @pl.loop(0, chunks)
     def _(m):
@@ -197,24 +244,98 @@
                     summed = value if j == 0 else summed + value
                 total[a + r] = summed
 
-        @pl.when(first)
-        def _():
-            for n, a in enumerate(starts(m)):
-                carry_copy(a, rows, 2 * m + n).start()
-
-    @pl.when(jnp.logical_not(first))
-    def _():
-        @pl.loop(0, chunks)
-        def _(m):
-            for n, a in enumerate(starts(m)):
-                carry_copy(a, rows, 2 * m + n).wait_recv()
-
-                @pl.when(has("lat", 1))
-                def _():
-                    @pl.loop(0, rows)
-                    def _(r):
-                        total[a + r] = total[a + r] + carried[a + r]
-                    carry_copy(a, rows, 2 * m + n).start()
+        for p in (2 * m, 2 * m + 1):
+            @pl.when(jnp.logical_and(at["lat"] == 0, p >= AROUND))
+            def _():
+                carry_copy(p).start()
+
+            @pl.when(jnp.logical_and(at["lat"] == last - 1, p < AROUND))
+            def _():
+                suffix_copy(p, total).start()
+
+    def add_suffix(p):
+        suffix_copy(p, suffix).wait_recv()
+
+        @pl.loop(0, rows)
+        def _(r):
+            i = span(p).start + r
+            suffix[i] = suffix[i] + total[i]
+
+    def pass_up(p):
+        carry_copy(p).wait_recv()
+
+        @pl.loop(0, rows)
+        def _(r):
+            i = span(p).start + r
+            total[i] = total[i] + carried[i]
+        carry_copy(p).start()
+
+    def take_off(p, own):
+        @pl.loop(0, rows)
+        def _(r):
+            i = span(p).start + r
+            carried[i] = whole[i] - own[i]
+
+    @block(0)
+    def _():
+        @pl.loop(RETURNED, AROUND)
+        def _(p):
+            carry_copy(p).start()
+
+        @pl.loop(0, AROUND)
+        def _(p):
+            add_suffix(p)
+            round_copy(p).start()
+
+    @block(1)
+    def _():
+        @pl.loop(0, AROUND)
+        def _(p):
+            add_suffix(p)
+            suffix_copy(p, suffix).start()
+            pass_up(AROUND + p)
+
+        @pl.loop(2 * AROUND, pieces)
+        def _(p):
+            pass_up(p)
+
+        @pl.loop(0, RETURNED)
+        def _(p):
+            whole_copy(p, whole).wait_recv()
+            take_off(p, suffix)
+
+        @pl.loop(RETURNED, AROUND)
+        def _(p):
+            carry_copy(p).wait_recv()
+
+    @block(2)
+    def _():
+        lead = pieces - 2 * AROUND
+
+        @pl.loop(AROUND, AROUND + lead)
+        def _(p):
+            pass_up(p)
+
+        @pl.loop(0, AROUND)
+        def _(p):
+            whole_copy(p, whole).wait_recv()
+
+            @pl.when(p < RETURNED)
+            def _():
+                whole_copy(p, whole).start()
+            take_off(p, total)
+            pass_up(AROUND + lead + p)
+
+    @block(3)
+    def _():
+        @pl.loop(0, AROUND)
+        def _(p):
+            carry_copy(p).wait_recv()
+            whole_copy(p, carried).start()
+
+        @pl.loop(AROUND, pieces)
+        def _(p):
+            carry_copy(p).wait_recv()
 
     for side in (0, 1):
         @pl.when(has("lat", side))
@@ -232,9 +353,27 @@
             for s in range(STEPS):
                 lev_copy(s, 0, ni, 0, side).wait_send()
 
-    @pl.when(has("lat", 1))
-    def _():
-        carry_copy(0, ni, 0).wait_send()
+    chain = pieces - AROUND
+
+    @block(0)
+    def _():
+        carry_copy(0, pieces - RETURNED).wait_send()
+        round_copy(0, AROUND).wait_send()
+
+    @block(1)
+    def _():
+        carry_copy(0, chain).wait_send()
+        suffix_copy(0, suffix, AROUND).wait_send()
+
+    @block(2)
+    def _():
+        carry_copy(0, chain).wait_send()
+        suffix_copy(0, total, AROUND).wait_send()
+        whole_copy(0, whole, RETURNED).wait_send()
+
+    @block(3)
+    def _():
+        whole_copy(0, carried, AROUND).wait_send()
 
 
 def march(tracer, crowding, rows):
@@ -253,12 +392,16 @@
             pltpu.VMEM((STEPS, 2, ni, nj, 1, levels), f32),
             pltpu.VMEM((STEPS, 2, ni, nj, 1, levels), f32),
             pltpu.VMEM((ni, nk, levels), f32),
+            pltpu.VMEM((ni, nk, levels), f32),
+            pltpu.VMEM((ni, nk, levels), f32),
             dma((2,)),
-            dma((7,)),
+            dma((10,)),
             dma((STEPS, chunks, 2)),
             dma((STEPS, 2)),
             dma((STEPS, chunks, 2)),
             dma((2 * chunks,)),
+            dma((AROUND,)),
+            dma((AROUND,)),
         ],
         compiler_params=pltpu.CompilerParams(
             collective_id=0, has_side_effects=True, vmem_limit_bytes=48 * 2**20),
@@ -266,25 +409,39 @@
     )(tracer, crowding)
 
 
-def sums_kernel(scale, end, carried, sums, copied):
-    run = carried[...]
-    for j in range(end.shape[0]):
-        value = end[j]
-        run = run + value
-        sums[j] = run * scale
-        copied[j] = value
+def sums_kernel(scale, block, end, carried, sums, copied, held, sem):
+    nj, ni = end.shape[:2]
+    blocks = ni // block
+
+    def written(n, b):
+        at_b = pl.ds(b * block, block)
+        source, target = ((end, copied), (held, sums))[n]
+        return pltpu.make_async_copy(source.at[:, at_b], target.at[:, at_b], sem.at[n, b])
+
+    for b in range(blocks):
+        written(0, b).start()
+    for b in range(blocks):
+        @pl.loop(b * block, (b + 1) * block)
+        def _(i):
+            run = carried[i]
+            for j in range(nj):
+                run = run + end[j, i]
+                held[j, i] = run * scale
+        written(1, b).start()
+    for b in range(blocks):
+        for n in (0, 1):
+            written(n, b).wait()
 
 
 def sums_along_j(end, carried, cells):
-    nj, ni, nk, levels = end.shape
+    ni = end.shape[1]
     block = min(8, ni)
-    whole = pl.BlockSpec((nj, block, nk, levels), lambda i: (0, i, 0, 0))
     return pl.pallas_call(
-        functools.partial(sums_kernel, 1.0 / cells),
-        grid=(ni // block,),
+        functools.partial(sums_kernel, 1.0 / cells, block),
         out_shape=(jax.ShapeDtypeStruct(end.shape, end.dtype),) * 2,
-        in_specs=[whole, pl.BlockSpec((block, nk, levels), lambda i: (i, 0, 0))],
-        out_specs=(whole, whole),
+        in_specs=[pl.BlockSpec(memory_space=pltpu.VMEM)] * 2,
+        out_specs=(pl.BlockSpec(memory_space=pl.ANY),) * 2,
+        scratch_shapes=[pltpu.VMEM(end.shape, end.dtype), pltpu.SemaphoreType.DMA((2, ni // block))],
         compiler_params=pltpu.CompilerParams(vmem_limit_bytes=12 * 2**20),
         name="sums",
     )(end, carried)

time: 135 us -> 125 us (0.926)
  the two profiles are of different devices: /device:TPU:30 before, /device:TPU:248 now
where the time goes in v2:
time: 125 us
  Pallas kernels  125 us (100%)
    pallas_call x1, Pallas kernels, march(): pl.pallas_call(functools.partial(march_kernel, rows), out_shape=(jax.Shap...  121 us
    pallas_call x1, Pallas kernels, sums_along_j(): pl.pallas_call(functools.partial(sums_kernel, 1.0 / cells, block), out_sh...  3.42 us

profile of v2, /device:TPU:248, one launch (start us, length us, event | category | flops | bytes accessed | tf_op | source)
XLA Modules:
  0.0 125.4 jit_solution(4521680015945277575)
XLA Ops:
  0.6 121.3 %march.1 = (f32[4,64,32,128]{3,2,1,0:T(8,128)S(1)}, f32[64,32,128]{2,1,0:T(8,128)S(1)}) custom-call(f32[4,64,32,128]{3,2,1,0:T(8,128)} %tracer.1, f32[4,64,32,128]{3,2,1,0:T(8,128)} %crowding.1), custom_call_target="tpu_custom_call" | custom-call | tf_op jit(solution)/shard_map/march/pallas_call | solution.py:384
  121.9 3.4 %sums.1 = (f32[4,64,32,128]{3,2,1,0:T(8,128)}, f32[4,64,32,128]{3,2,1,0:T(8,128)}) custom-call(f32[4,64,32,128]{3,2,1,0:T(8,128)S(1)} %get-tuple-element.4.end, f32[64,32,128]{2,1,0:T(8,128)S(1)} %get-tuple-element.5.carried), custom_call_target="tpu_custom_call" | custom-call | tf_op jit(solution)/shard_map/sums/pallas_call | solution.py:439

commit v3 on v2

--- a/solution.py
+++ b/solution.py
@@ -9,14 +9,17 @@
 
 STEPS = 4
 ROWS = 4
-AROUND = 6
-RETURNED = 3
+PIECE = 2
+AROUND = 14
+RETURNED = 8
+LEAD = 9
 MESH = pl.DeviceIdType.MESH
 AXES = ("unit", "lat", "lon", "lev")
 
 
 def march_kernel(rows, tracer, crowding, end, carried, t, c, faces, edges, total, suffix, whole,
-                 load_sem, send_sem, lat_sem, lon_sem, lev_sem, carry_sem, suffix_sem, whole_sem):
+                 load_sem, send_sem, lat_sem, lon_sem, lev_sem, carry_sem, suffix_sem, whole_sem,
+                 go_sem):
     nj, ni, nk, levels = tracer.shape
     chunks = ni // (2 * rows)
     at = {axis: lax.axis_index(axis) for axis in AXES}
@@ -51,33 +54,37 @@
             faces.at[s, side, pl.ds(a, length)], edges.at[s, 1 - side, pl.ds(a, length)],
             send_sem.at[4 + side], lev_sem.at[s, m, 1 - side], device_id=there("lev", side), device_id_type=MESH)
 
-    pieces = 2 * chunks
+    piece = min(PIECE, rows)
+    half = rows // piece
+    pieces = 2 * half * chunks
+    assert 2 * AROUND <= pieces <= 2 * AROUND + LEAD
     last = size["lat"] - 1
 
-    def span(p, count=1):
-        m = p // 2
-        return pl.ds(jnp.where(p % 2 == 0, m * rows, ni - (m + 1) * rows), count * rows)
+    def span(p):
+        m, n = p // (2 * half), p % (2 * half)
+        start = jnp.where(n < half, m * rows, ni - (m + 1) * rows - rows)
+        return pl.ds(start + n * piece, piece)
 
     def carry_copy(p, count=1):
-        at_p = span(p) if count == 1 else pl.ds(0, count * rows)
+        at_p = span(p) if count == 1 else pl.ds(0, count * piece)
         return pltpu.make_async_remote_copy(
             total.at[at_p], carried.at[at_p], send_sem.at[6], carry_sem.at[p],
             device_id=there("lat", 1), device_id_type=MESH)
 
     def suffix_copy(p, source, count=1):
-        at_p = span(p) if count == 1 else pl.ds(0, count * rows)
+        at_p = span(p) if count == 1 else pl.ds(0, count * piece)
         return pltpu.make_async_remote_copy(
             source.at[at_p], suffix.at[at_p], send_sem.at[7], suffix_sem.at[p],
             device_id=there("lat", 0), device_id_type=MESH)
 
     def round_copy(p, count=1):
-        at_p = span(p) if count == 1 else pl.ds(0, count * rows)
+        at_p = span(p) if count == 1 else pl.ds(0, count * piece)
         return pltpu.make_async_remote_copy(
             suffix.at[at_p], carried.at[at_p], send_sem.at[8], carry_sem.at[p],
             device_id={"lat": last}, device_id_type=MESH)
 
     def whole_copy(p, source, count=1):
-        at_p = span(p) if count == 1 else pl.ds(0, count * rows)
+        at_p = span(p) if count == 1 else pl.ds(0, count * piece)
         return pltpu.make_async_remote_copy(
             source.at[at_p], whole.at[at_p], send_sem.at[9], whole_sem.at[p],
             device_id=there("lat", 0), device_id_type=MESH)
@@ -87,15 +94,25 @@
 
     barrier = pltpu.get_barrier_semaphore()
 
-    def greet(axis, side, where=None):
-        pl.semaphore_signal(
-            barrier, inc=1, device_id=there(axis, side) if where is None else where, device_id_type=MESH)
-
+    def greet(where):
+        pl.semaphore_signal(barrier, inc=1, device_id=where, device_id_type=MESH)
+
+    def let_go(where):
+        pl.semaphore_signal(go_sem, inc=1, device_id=where, device_id_type=MESH)
+
+    def count(axis):
+        return has(axis, 0).astype(jnp.int32) + has(axis, 1).astype(jnp.int32)
+
+    odd = at["lev"] % 2 == 1
+    even = at["lev"] % 2 == 0
+    keeper = jnp.logical_and(even, at["lat"] == last)
+    ends = jnp.logical_or(at["lat"] == 0, at["lat"] == last)
+    between = jnp.logical_and(at["lat"] > 0, at["lat"] < last - 1)
     for axis in ("lat", "lon"):
         for side in (0, 1):
-            pl.when(has(axis, side))(functools.partial(greet, axis, side))
-    ends = jnp.logical_or(at["lat"] == 0, at["lat"] == last)
-    pl.when(ends)(functools.partial(greet, "lat", 0, {"lat": last - at["lat"]}))
+            pl.when(has(axis, side))(functools.partial(greet, there(axis, side)))
+    pl.when(ends)(functools.partial(greet, {"lat": last - at["lat"]}))
+    pl.when(jnp.logical_and(even, between))(functools.partial(greet, {"lat": last}))
     load_t.start()
     load_c.start()
 
@@ -127,12 +144,12 @@
                     for j in range(nj):
                         edges[s, side, i, j] = jnp.zeros((1, levels), jnp.float32)
 
-    def count(axis):
-        return has(axis, 0).astype(jnp.int32) + has(axis, 1).astype(jnp.int32)
-
-    odd = at["lev"] % 2 == 1
     near = count("lat") + count("lon") + ends.astype(jnp.int32)
-    pl.semaphore_wait(barrier, near + jnp.where(odd, 0, count("lev")))
+    pl.semaphore_wait(
+        barrier, near + jnp.where(keeper, last - 2 + size["lat"] * count("lev"), 0))
+    for side in (0, 1):
+        pl.when(jnp.logical_and(odd, has("lev", side)))(
+            functools.partial(greet, {"lat": last, **there("lev", side)}))
 
     for m in range(chunks):
         for side in (0, 1):
@@ -146,8 +163,17 @@
         def _():
             lon_copy(0, side, tracer.at[:, 0 if side == 0 else ni - 1]).start()
 
+    @pl.when(keeper)
+    def _():
+        for n in range(last):
+            let_go({"lat": n})
+
+    @pl.when(jnp.logical_and(even, at["lat"] < last))
+    def _():
+        pl.semaphore_wait(go_sem, 1)
+
     for side in (0, 1):
-        pl.when(has("lev", side))(functools.partial(greet, "lev", side))
+        pl.when(jnp.logical_and(even, has("lev", side)))(functools.partial(let_go, there("lev", side)))
 
     def send_lev(s, m):
         for side in (0, 1):
@@ -169,7 +195,7 @@
 
     @pl.when(odd)
     def _():
-        pl.semaphore_wait(barrier, count("lev"))
+        pl.semaphore_wait(go_sem, count("lev"))
 
     @pl.loop(0, chunks)
     def _(m):
@@ -244,7 +270,9 @@
                     summed = value if j == 0 else summed + value
                 total[a + r] = summed
 
-        for p in (2 * m, 2 * m + 1):
+        for n in range(2 * half):
+            p = 2 * half * m + n
+
             @pl.when(jnp.logical_and(at["lat"] == 0, p >= AROUND))
             def _():
                 carry_copy(p).start()
@@ -256,23 +284,20 @@
     def add_suffix(p):
         suffix_copy(p, suffix).wait_recv()
 
-        @pl.loop(0, rows)
-        def _(r):
+        for r in range(piece):
             i = span(p).start + r
             suffix[i] = suffix[i] + total[i]
 
     def pass_up(p):
         carry_copy(p).wait_recv()
 
-        @pl.loop(0, rows)
-        def _(r):
+        for r in range(piece):
             i = span(p).start + r
             total[i] = total[i] + carried[i]
         carry_copy(p).start()
 
     def take_off(p, own):
-        @pl.loop(0, rows)
-        def _(r):
+        for r in range(piece):
             i = span(p).start + r
             carried[i] = whole[i] - own[i]
 
@@ -310,21 +335,28 @@
 
     @block(2)
     def _():
-        lead = pieces - 2 * AROUND
-
-        @pl.loop(AROUND, AROUND + lead)
-        def _(p):
-            pass_up(p)
-
-        @pl.loop(0, AROUND)
-        def _(p):
+        paired = pieces - AROUND - LEAD
+
+        def take_whole(p):
             whole_copy(p, whole).wait_recv()
 
             @pl.when(p < RETURNED)
             def _():
                 whole_copy(p, whole).start()
             take_off(p, total)
-            pass_up(AROUND + lead + p)
+
+        @pl.loop(AROUND, AROUND + LEAD)
+        def _(p):
+            pass_up(p)
+
+        @pl.loop(0, paired)
+        def _(p):
+            pass_up(AROUND + LEAD + p)
+            take_whole(p)
+
+        @pl.loop(paired, AROUND)
+        def _(p):
+            take_whole(p)
 
     @block(3)
     def _():
@@ -399,9 +431,10 @@
             dma((STEPS, chunks, 2)),
             dma((STEPS, 2)),
             dma((STEPS, chunks, 2)),
-            dma((2 * chunks,)),
+            dma((ni // min(PIECE, rows),)),
             dma((AROUND,)),
             dma((AROUND,)),
+            pltpu.SemaphoreType.REGULAR,
         ],
         compiler_params=pltpu.CompilerParams(
             collective_id=0, has_side_effects=True, vmem_limit_bytes=48 * 2**20),

time: 125 us -> 120 us (0.960)
  the two profiles are of different devices: /device:TPU:248 before, /device:TPU:30 now
where the time goes in v3:
time: 120 us; the launch traced here: 119 us
  Pallas kernels  118 us (98%)
    pallas_call x1, Pallas kernels, march(): pl.pallas_call(functools.partial(march_kernel, rows), out_shape=(jax.Shap...  115 us
    pallas_call x1, Pallas kernels, sums_along_j(): pl.pallas_call(functools.partial(sums_kernel, 1.0 / cells, block), out_sh...  3.42 us

profile of v3, /device:TPU:30, one launch (start us, length us, event | category | flops | bytes accessed | tf_op | source)
XLA Modules:
  0.0 118.9 jit_solution(10783641795328573578)
XLA Ops:
  0.6 114.8 %march.1 = (f32[4,64,32,128]{3,2,1,0:T(8,128)S(1)}, f32[64,32,128]{2,1,0:T(8,128)S(1)}) custom-call(f32[4,64,32,128]{3,2,1,0:T(8,128)} %tracer.1, f32[4,64,32,128]{3,2,1,0:T(8,128)} %crowding.1), custom_call_target="tpu_custom_call" | custom-call | tf_op jit(solution)/shard_map/march/pallas_call | solution.py:416
  115.4 3.4 %sums.1 = (f32[4,64,32,128]{3,2,1,0:T(8,128)}, f32[4,64,32,128]{3,2,1,0:T(8,128)}) custom-call(f32[4,64,32,128]{3,2,1,0:T(8,128)S(1)} %get-tuple-element.4.end, f32[64,32,128]{2,1,0:T(8,128)S(1)} %get-tuple-element.5.carried), custom_call_target="tpu_custom_call" | custom-call | tf_op jit(solution)/shard_map/sums/pallas_call | solution.py:472

commit v4 on v3

--- a/solution.py
+++ b/solution.py
@@ -10,9 +10,11 @@
 STEPS = 4
 ROWS = 4
 PIECE = 2
-AROUND = 14
-RETURNED = 8
-LEAD = 9
+SPLIT = 7
+ROUND = 14
+CHAIN = 18
+RETURNED = 10
+LEAD = 5
 MESH = pl.DeviceIdType.MESH
 AXES = ("unit", "lat", "lon", "lev")
 
@@ -57,7 +59,7 @@
     piece = min(PIECE, rows)
     half = rows // piece
     pieces = 2 * half * chunks
-    assert 2 * AROUND <= pieces <= 2 * AROUND + LEAD
+    assert CHAIN - SPLIT <= pieces - CHAIN <= ROUND + LEAD
     last = size["lat"] - 1
 
     def span(p):
@@ -80,13 +82,13 @@
     def round_copy(p, count=1):
         at_p = span(p) if count == 1 else pl.ds(0, count * piece)
         return pltpu.make_async_remote_copy(
-            suffix.at[at_p], carried.at[at_p], send_sem.at[8], carry_sem.at[p],
+            suffix.at[at_p], whole.at[at_p], send_sem.at[8], whole_sem.at[p],
             device_id={"lat": last}, device_id_type=MESH)
 
-    def whole_copy(p, source, count=1):
+    def whole_copy(p, count=1):
         at_p = span(p) if count == 1 else pl.ds(0, count * piece)
         return pltpu.make_async_remote_copy(
-            source.at[at_p], whole.at[at_p], send_sem.at[9], whole_sem.at[p],
+            whole.at[at_p], whole.at[at_p], send_sem.at[9], whole_sem.at[p],
             device_id=there("lat", 0), device_id_type=MESH)
 
     load_t = pltpu.make_async_copy(tracer, t.at[0, pl.ds(1, nj), pl.ds(1, ni)], load_sem.at[0])
@@ -273,99 +275,133 @@
         for n in range(2 * half):
             p = 2 * half * m + n
 
-            @pl.when(jnp.logical_and(at["lat"] == 0, p >= AROUND))
+            up = jnp.logical_or(jnp.logical_and(at["lat"] == 0, p >= CHAIN),
+                                jnp.logical_and(at["lat"] == 2, p < SPLIT))
+            down = jnp.logical_or(jnp.logical_and(at["lat"] == 1, p < SPLIT),
+                                  jnp.logical_and(at["lat"] == 2, jnp.logical_and(p >= SPLIT, p < CHAIN)))
+
+            @pl.when(up)
             def _():
                 carry_copy(p).start()
 
-            @pl.when(jnp.logical_and(at["lat"] == last - 1, p < AROUND))
+            @pl.when(down)
             def _():
                 suffix_copy(p, total).start()
+
+    def combine(p, target, value):
+        for r in range(piece):
+            i = span(p).start + r
+            target[i] = value(i)
 
     def add_suffix(p):
         suffix_copy(p, suffix).wait_recv()
-
-        for r in range(piece):
-            i = span(p).start + r
-            suffix[i] = suffix[i] + total[i]
+        combine(p, suffix, lambda i: suffix[i] + total[i])
 
     def pass_up(p):
         carry_copy(p).wait_recv()
-
-        for r in range(piece):
-            i = span(p).start + r
-            total[i] = total[i] + carried[i]
+        combine(p, total, lambda i: total[i] + carried[i])
         carry_copy(p).start()
 
-    def take_off(p, own):
-        for r in range(piece):
-            i = span(p).start + r
-            carried[i] = whole[i] - own[i]
-
     @block(0)
     def _():
-        @pl.loop(RETURNED, AROUND)
+        @pl.loop(ROUND, CHAIN)
         def _(p):
             carry_copy(p).start()
 
-        @pl.loop(0, AROUND)
+        @pl.loop(RETURNED, ROUND)
+        def _(p):
+            carry_copy(p).start()
+
+        @pl.loop(0, CHAIN)
         def _(p):
             add_suffix(p)
             round_copy(p).start()
 
     @block(1)
     def _():
-        @pl.loop(0, AROUND)
+        @pl.loop(SPLIT, CHAIN)
         def _(p):
             add_suffix(p)
             suffix_copy(p, suffix).start()
-            pass_up(AROUND + p)
-
-        @pl.loop(2 * AROUND, pieces)
+            pass_up(CHAIN - SPLIT + p)
+
+        @pl.loop(2 * CHAIN - SPLIT, pieces)
         def _(p):
             pass_up(p)
 
-        @pl.loop(0, RETURNED)
-        def _(p):
-            whole_copy(p, whole).wait_recv()
-            take_off(p, suffix)
-
-        @pl.loop(RETURNED, AROUND)
+        @pl.loop(ROUND, CHAIN)
+        def _(p):
+            pass_up(p)
+
+        @pl.loop(0, SPLIT)
+        def _(p):
+            whole_copy(p).wait_recv()
+            combine(p, carried, lambda i: whole[i] - total[i])
+
+        @pl.loop(SPLIT, RETURNED)
+        def _(p):
+            whole_copy(p).wait_recv()
+            combine(p, carried, lambda i: whole[i] - suffix[i])
+
+        @pl.loop(RETURNED, ROUND)
         def _(p):
             carry_copy(p).wait_recv()
 
     @block(2)
     def _():
-        paired = pieces - AROUND - LEAD
+        paired = pieces - CHAIN - LEAD
 
         def take_whole(p):
-            whole_copy(p, whole).wait_recv()
+            whole_copy(p).wait_recv()
 
             @pl.when(p < RETURNED)
             def _():
-                whole_copy(p, whole).start()
-            take_off(p, total)
-
-        @pl.loop(AROUND, AROUND + LEAD)
+                whole_copy(p).start()
+
+            @pl.when(p < SPLIT)
+            def _():
+                combine(p, carried, lambda i: whole[i])
+
+            @pl.when(p >= SPLIT)
+            def _():
+                combine(p, carried, lambda i: whole[i] - total[i])
+
+        @pl.loop(CHAIN, CHAIN + LEAD)
         def _(p):
             pass_up(p)
 
         @pl.loop(0, paired)
         def _(p):
-            pass_up(AROUND + LEAD + p)
+            pass_up(CHAIN + LEAD + p)
             take_whole(p)
 
-        @pl.loop(paired, AROUND)
+        @pl.loop(paired, ROUND)
         def _(p):
             take_whole(p)
 
+        @pl.loop(ROUND, CHAIN)
+        def _(p):
+            carry_copy(p).wait_recv()
+
     @block(3)
     def _():
-        @pl.loop(0, AROUND)
-        def _(p):
+        @pl.loop(0, SPLIT)
+        def _(p):
+            whole_copy(p).wait_recv()
+            whole_copy(p).start()
             carry_copy(p).wait_recv()
-            whole_copy(p, carried).start()
-
-        @pl.loop(AROUND, pieces)
+            combine(p, carried, lambda i: carried[i] + whole[i])
+
+        @pl.loop(SPLIT, CHAIN)
+        def _(p):
+            whole_copy(p).wait_recv()
+
+            @pl.when(p < ROUND)
+            def _():
+                whole_copy(p).start()
+            combine(p, carried, lambda i: whole[i])
+
+        @pl.loop(CHAIN, pieces)
         def _(p):
             carry_copy(p).wait_recv()
 
@@ -385,27 +421,27 @@
             for s in range(STEPS):
                 lev_copy(s, 0, ni, 0, side).wait_send()
 
-    chain = pieces - AROUND
+    chain = pieces - CHAIN
 
     @block(0)
     def _():
-        carry_copy(0, pieces - RETURNED).wait_send()
-        round_copy(0, AROUND).wait_send()
+        carry_copy(0, chain + CHAIN - RETURNED).wait_send()
+        round_copy(0, CHAIN).wait_send()
 
     @block(1)
     def _():
-        carry_copy(0, chain).wait_send()
-        suffix_copy(0, suffix, AROUND).wait_send()
+        carry_copy(0, chain + CHAIN - ROUND).wait_send()
+        suffix_copy(0, suffix, CHAIN).wait_send()
 
     @block(2)
     def _():
-        carry_copy(0, chain).wait_send()
-        suffix_copy(0, total, AROUND).wait_send()
-        whole_copy(0, whole, RETURNED).wait_send()
+        carry_copy(0, chain + SPLIT).wait_send()
+        suffix_copy(0, total, CHAIN - SPLIT).wait_send()
+        whole_copy(0, RETURNED).wait_send()
 
     @block(3)
     def _():
-        whole_copy(0, carried, AROUND).wait_send()
+        whole_copy(0, ROUND).wait_send()
 
 
 def march(tracer, crowding, rows):
@@ -432,8 +468,8 @@
             dma((STEPS, 2)),
             dma((STEPS, chunks, 2)),
             dma((ni // min(PIECE, rows),)),
-            dma((AROUND,)),
-            dma((AROUND,)),
+            dma((CHAIN,)),
+            dma((CHAIN,)),
             pltpu.SemaphoreType.REGULAR,
         ],
         compiler_params=pltpu.CompilerParams(

time: 120 us -> 118 us (0.983)
  Pallas kernels: 118 us -> 116 us
    pallas_call x1, Pallas kernels: 115 us -> 112 us  [march(): pl.pallas_call(functools.partial(march_kernel, rows), out_shape=(jax.Shap...]
where the time goes in v4:
time: 118 us; the launch traced here: 116 us
  Pallas kernels  116 us (98%)
    pallas_call x1, Pallas kernels, march(): pl.pallas_call(functools.partial(march_kernel, rows), out_shape=(jax.Shap...  112 us
    pallas_call x1, Pallas kernels, sums_along_j(): pl.pallas_call(functools.partial(sums_kernel, 1.0 / cells, block), out_sh...  3.42 us

profile of v4, /device:TPU:30, one launch (start us, length us, event | category | flops | bytes accessed | tf_op | source)
XLA Modules:
  0.0 116.4 jit_solution(1892053562386155404)
XLA Ops:
  0.6 112.4 %march.1 = (f32[4,64,32,128]{3,2,1,0:T(8,128)S(1)}, f32[64,32,128]{2,1,0:T(8,128)S(1)}) custom-call(f32[4,64,32,128]{3,2,1,0:T(8,128)} %tracer.1, f32[4,64,32,128]{3,2,1,0:T(8,128)} %crowding.1), custom_call_target="tpu_custom_call" | custom-call | tf_op jit(solution)/shard_map/march/pallas_call | solution.py:452
  113.0 3.4 %sums.1 = (f32[4,64,32,128]{3,2,1,0:T(8,128)}, f32[4,64,32,128]{3,2,1,0:T(8,128)}) custom-call(f32[4,64,32,128]{3,2,1,0:T(8,128)S(1)} %get-tuple-element.4.end, f32[64,32,128]{2,1,0:T(8,128)S(1)} %get-tuple-element.5.carried), custom_call_target="tpu_custom_call" | custom-call | tf_op jit(solution)/shard_map/sums/pallas_call | solution.py:508

commit v5 on v4

--- a/solution.py
+++ b/solution.py
@@ -8,12 +8,12 @@
 from jax.sharding import PartitionSpec as P
 
 STEPS = 4
-ROWS = 4
+ROWS = 8
 PIECE = 2
-SPLIT = 7
+SPLIT = 8
 ROUND = 14
-CHAIN = 18
-RETURNED = 10
+CHAIN = 19
+RETURNED = 9
 LEAD = 5
 MESH = pl.DeviceIdType.MESH
 AXES = ("unit", "lat", "lon", "lev")
@@ -118,34 +118,6 @@
     load_t.start()
     load_c.start()
 
-    zero = jnp.zeros((nk, levels), jnp.float32)
-    for side in (0, 1):
-        @pl.when(jnp.logical_not(has("lat", side)))
-        def _():
-            @pl.loop(0, ni)
-            def _(i):
-                for s in range(STEPS):
-                    t[s, 0 if side == 0 else nj + 1, 1 + i] = zero
-
-            if side == 0:
-                @pl.loop(0, ni)
-                def _(i):
-                    carried[i] = zero
-
-        @pl.when(jnp.logical_not(has("lon", side)))
-        def _():
-            for s in range(STEPS):
-                for j in range(nj):
-                    t[s, 1 + j, 0 if side == 0 else ni + 1] = zero
-
-        @pl.when(jnp.logical_not(has("lev", side)))
-        def _():
-            @pl.loop(0, ni)
-            def _(i):
-                for s in range(STEPS):
-                    for j in range(nj):
-                        edges[s, side, i, j] = jnp.zeros((1, levels), jnp.float32)
-
     near = count("lat") + count("lon") + ends.astype(jnp.int32)
     pl.semaphore_wait(
         barrier, near + jnp.where(keeper, last - 2 + size["lat"] * count("lev"), 0))
@@ -169,6 +141,34 @@
     def _():
         for n in range(last):
             let_go({"lat": n})
+
+    zero = jnp.zeros((nk, levels), jnp.float32)
+    for side in (0, 1):
+        @pl.when(jnp.logical_not(has("lat", side)))
+        def _():
+            @pl.loop(0, ni)
+            def _(i):
+                for s in range(STEPS):
+                    t[s, 0 if side == 0 else nj + 1, 1 + i] = zero
+
+            if side == 0:
+                @pl.loop(0, ni)
+                def _(i):
+                    carried[i] = zero
+
+        @pl.when(jnp.logical_not(has("lon", side)))
+        def _():
+            for s in range(STEPS):
+                for j in range(nj):
+                    t[s, 1 + j, 0 if side == 0 else ni + 1] = zero
+
+        @pl.when(jnp.logical_not(has("lev", side)))
+        def _():
+            @pl.loop(0, ni)
+            def _(i):
+                for s in range(STEPS):
+                    for j in range(nj):
+                        edges[s, side, i, j] = jnp.zeros((1, levels), jnp.float32)
 
     @pl.when(jnp.logical_and(even, at["lat"] < last))
     def _():

time: 118 us -> 117 us (level)
    pallas_call x1, Pallas kernels: 112 us -> 111 us  [march(): pl.pallas_call(functools.partial(march_kernel, rows), out_shape=(jax.Shap...]
where the time goes in v5:
time: 117 us; the launch traced here: 115 us
  Pallas kernels  115 us (98%)
    pallas_call x1, Pallas kernels, march(): pl.pallas_call(functools.partial(march_kernel, rows), out_shape=(jax.Shap...  111 us
    pallas_call x1, Pallas kernels, sums_along_j(): pl.pallas_call(functools.partial(sums_kernel, 1.0 / cells, block), out_sh...  3.42 us

profile of v5, /device:TPU:30, one launch (start us, length us, event | category | flops | bytes accessed | tf_op | source)
XLA Modules:
  0.0 115.2 jit_solution(499387519986038680)
XLA Ops:
  0.6 111.1 %march.1 = (f32[4,64,32,128]{3,2,1,0:T(8,128)S(1)}, f32[64,32,128]{2,1,0:T(8,128)S(1)}) custom-call(f32[4,64,32,128]{3,2,1,0:T(8,128)} %tracer.1, f32[4,64,32,128]{3,2,1,0:T(8,128)} %crowding.1), custom_call_target="tpu_custom_call" | custom-call | tf_op jit(solution)/shard_map/march/pallas_call | solution.py:452
  111.7 3.4 %sums.1 = (f32[4,64,32,128]{3,2,1,0:T(8,128)}, f32[4,64,32,128]{3,2,1,0:T(8,128)}) custom-call(f32[4,64,32,128]{3,2,1,0:T(8,128)S(1)} %get-tuple-element.4.end, f32[64,32,128]{2,1,0:T(8,128)S(1)} %get-tuple-element.5.carried), custom_call_target="tpu_custom_call" | custom-call | tf_op jit(solution)/shard_map/sums/pallas_call | solution.py:508

commit v6 on v5

--- a/solution.py
+++ b/solution.py
@@ -14,7 +14,7 @@
 ROUND = 14
 CHAIN = 19
 RETURNED = 9
-LEAD = 5
+LEAD = 4
 MESH = pl.DeviceIdType.MESH
 AXES = ("unit", "lat", "lon", "lev")
 
@@ -64,6 +64,8 @@
 
     def span(p):
         m, n = p // (2 * half), p % (2 * half)
+        if isinstance(p, int):
+            return pl.ds((m * rows if n < half else ni - (m + 1) * rows - rows) + n * piece, piece)
         start = jnp.where(n < half, m * rows, ni - (m + 1) * rows - rows)
         return pl.ds(start + n * piece, piece)
 
@@ -302,48 +304,54 @@
         combine(p, total, lambda i: total[i] + carried[i])
         carry_copy(p).start()
 
+    def unrolled(start, stop):
+        def run(body):
+            for p in range(start, stop):
+                body(p)
+        return run
+
     @block(0)
     def _():
-        @pl.loop(ROUND, CHAIN)
+        @unrolled(ROUND, CHAIN)
         def _(p):
             carry_copy(p).start()
 
-        @pl.loop(RETURNED, ROUND)
+        @unrolled(RETURNED, ROUND)
         def _(p):
             carry_copy(p).start()
 
-        @pl.loop(0, CHAIN)
+        @unrolled(0, CHAIN)
         def _(p):
             add_suffix(p)
             round_copy(p).start()
 
     @block(1)
     def _():
-        @pl.loop(SPLIT, CHAIN)
-        def _(p):
+        @unrolled(SPLIT, CHAIN)
+        def _(p):
+            pass_up(CHAIN - SPLIT + p)
             add_suffix(p)
             suffix_copy(p, suffix).start()
-            pass_up(CHAIN - SPLIT + p)
-
-        @pl.loop(2 * CHAIN - SPLIT, pieces)
+
+        @unrolled(2 * CHAIN - SPLIT, pieces)
         def _(p):
             pass_up(p)
 
-        @pl.loop(ROUND, CHAIN)
+        @unrolled(ROUND, CHAIN)
         def _(p):
             pass_up(p)
 
-        @pl.loop(0, SPLIT)
+        @unrolled(0, SPLIT)
         def _(p):
             whole_copy(p).wait_recv()
             combine(p, carried, lambda i: whole[i] - total[i])
 
-        @pl.loop(SPLIT, RETURNED)
+        @unrolled(SPLIT, RETURNED)
         def _(p):
             whole_copy(p).wait_recv()
             combine(p, carried, lambda i: whole[i] - suffix[i])
 
-        @pl.loop(RETURNED, ROUND)
+        @unrolled(RETURNED, ROUND)
         def _(p):
             carry_copy(p).wait_recv()
 
@@ -366,33 +374,33 @@
             def _():
                 combine(p, carried, lambda i: whole[i] - total[i])
 
-        @pl.loop(CHAIN, CHAIN + LEAD)
+        @unrolled(CHAIN, CHAIN + LEAD)
         def _(p):
             pass_up(p)
 
-        @pl.loop(0, paired)
+        @unrolled(0, paired)
         def _(p):
             pass_up(CHAIN + LEAD + p)
             take_whole(p)
 
-        @pl.loop(paired, ROUND)
+        @unrolled(paired, ROUND)
         def _(p):
             take_whole(p)
 
-        @pl.loop(ROUND, CHAIN)
+        @unrolled(ROUND, CHAIN)
         def _(p):
             carry_copy(p).wait_recv()
 
     @block(3)
     def _():
-        @pl.loop(0, SPLIT)
+        @unrolled(0, SPLIT)
         def _(p):
             whole_copy(p).wait_recv()
             whole_copy(p).start()
             carry_copy(p).wait_recv()
             combine(p, carried, lambda i: carried[i] + whole[i])
 
-        @pl.loop(SPLIT, CHAIN)
+        @unrolled(SPLIT, CHAIN)
         def _(p):
             whole_copy(p).wait_recv()
 
@@ -401,7 +409,7 @@
                 whole_copy(p).start()
             combine(p, carried, lambda i: whole[i])
 
-        @pl.loop(CHAIN, pieces)
+        @unrolled(CHAIN, pieces)
         def _(p):
             carry_copy(p).wait_recv()
 

time: 117 us -> 117 us (level)
  no operation moved by 1% of the time
where the time goes in v6:
time: 117 us; the launch traced here: 115 us
  Pallas kernels  115 us (98%)
    pallas_call x1, Pallas kernels, march(): pl.pallas_call(functools.partial(march_kernel, rows), out_shape=(jax.Shap...  111 us
    pallas_call x1, Pallas kernels, sums_along_j(): pl.pallas_call(functools.partial(sums_kernel, 1.0 / cells, block), out_sh...  3.42 us

profile of v6, /device:TPU:30, one launch (start us, length us, event | category | flops | bytes accessed | tf_op | source)
XLA Modules:
  0.0 115.2 jit_solution(1195739791708053801)
XLA Ops:
  0.6 111.1 %march.1 = (f32[4,64,32,128]{3,2,1,0:T(8,128)S(1)}, f32[64,32,128]{2,1,0:T(8,128)S(1)}) custom-call(f32[4,64,32,128]{3,2,1,0:T(8,128)} %tracer.1, f32[4,64,32,128]{3,2,1,0:T(8,128)} %crowding.1), custom_call_target="tpu_custom_call" | custom-call | tf_op jit(solution)/shard_map/march/pallas_call | solution.py:460
  111.7 3.4 %sums.1 = (f32[4,64,32,128]{3,2,1,0:T(8,128)}, f32[4,64,32,128]{3,2,1,0:T(8,128)}) custom-call(f32[4,64,32,128]{3,2,1,0:T(8,128)S(1)} %get-tuple-element.4.end, f32[64,32,128]{2,1,0:T(8,128)S(1)} %get-tuple-element.5.carried), custom_call_target="tpu_custom_call" | custom-call | tf_op jit(solution)/shard_map/sums/pallas_call | solution.py:516

commit v7 on v6

--- a/solution.py
+++ b/solution.py
@@ -31,7 +31,7 @@
         return at[axis] > 0 if side == 0 else at[axis] < size[axis] - 1
 
     def there(axis, side):
-        return {axis: at[axis] - 1 if side == 0 else at[axis] + 1}
+        return {axis: lax.rem(at[axis] + (size[axis] - 1 if side == 0 else 1), size[axis])}
 
     def starts(m):
         return (m * rows, ni - (m + 1) * rows)

time: 117 us -> 117 us (level)
  no operation moved by 1% of the time
where the time goes in v7:
time: 117 us; the launch traced here: 115 us
  Pallas kernels  115 us (98%)
    pallas_call x1, Pallas kernels, march(): pl.pallas_call(functools.partial(march_kernel, rows), out_shape=(jax.Shap...  111 us
    pallas_call x1, Pallas kernels, sums_along_j(): pl.pallas_call(functools.partial(sums_kernel, 1.0 / cells, block), out_sh...  3.42 us

profile of v7, /device:TPU:30, one launch (start us, length us, event | category | flops | bytes accessed | tf_op | source)
XLA Modules:
  0.0 115.2 jit_solution(13425620939430989973)
XLA Ops:
  0.6 111.1 %march.1 = (f32[4,64,32,128]{3,2,1,0:T(8,128)S(1)}, f32[64,32,128]{2,1,0:T(8,128)S(1)}) custom-call(f32[4,64,32,128]{3,2,1,0:T(8,128)} %tracer.1, f32[4,64,32,128]{3,2,1,0:T(8,128)} %crowding.1), custom_call_target="tpu_custom_call" | custom-call | tf_op jit(solution)/shard_map/march/pallas_call | solution.py:460
  111.7 3.4 %sums.1 = (f32[4,64,32,128]{3,2,1,0:T(8,128)}, f32[4,64,32,128]{3,2,1,0:T(8,128)}) custom-call(f32[4,64,32,128]{3,2,1,0:T(8,128)S(1)} %get-tuple-element.4.end, f32[64,32,128]{2,1,0:T(8,128)S(1)} %get-tuple-element.5.carried), custom_call_target="tpu_custom_call" | custom-call | tf_op jit(solution)/shard_map/sums/pallas_call | solution.py:516
